TPU v7x, 32 devices: a whole 2x2x4 slice. The times are simulated.
32 devices in a mesh: groups: 2 (over x), ctx: 16 (over z, y, core), tp: 1.
Axes of the slice: x: 2, y: 2, z: 4, core: 2. Of those that a mesh axis runs over, the one named last changes fastest.
Arguments:
- query_states: bfloat16 [8192, 32, 128], P(('groups', 'ctx'), 'tp'), parts along dimension 0, may hold values from -8 to 8
- key_states: bfloat16 [8192, 4, 128], P(('groups', 'ctx'), 'tp'), parts along dimension 0, may hold values from -8 to 8
- value_rows: bfloat16 [8192, 4, 128], P(('groups', 'ctx'), 'tp'), parts along dimension 0, may hold values from -12 to 12
- positions: int32 [8192], P(('groups', 'ctx')), parts along dimension 0, may hold values from 0 to 4095, as said below
- out_weight: bfloat16 [4096, 4096], P('tp', 'ctx'), may hold values from -0.375 to 0.375
Outputs:
- projected: bfloat16 [8192, 4096], P(('groups', 'ctx'), 'tp'), parts along dimension 0
There are 2 independent parts, one for each index of `groups`. A program takes and returns all parts, laid end to end along the dimension named above; an argument that names none is the same for every part. Nothing has to cross between parts.
Inputs may be any that keep to these rules, and one draw needn't show every extreme that they name: Each of 0 to 4095 appears once. Half-block b holds positions b * 128 to (b + 1) * 128 - 1. The 256 rows of one device along ctx hold half-block j and then half-block 32 - 1 - j, each in rising order, for a j below 16 that differs from device to device.
All inputs are finite; a program needn't handle non-finite values.
Results may differ from a plain program's by a relative error of at most 0.01.
Values may be sent and summed in bfloat16 or wider, within the bound.
A program may use at most 128 MiB of HBM per device.

v0:
```python
import jax
import jax.numpy as jnp
from jax import lax
from jax.sharding import PartitionSpec as P

LOW_START = -1e30


def for_sending(value):
    return jax.tree.map(lambda a: a.astype(jnp.bfloat16) if a.dtype == jnp.float32 else a, value)


def from_behind(value, axis, by):
    devices = lax.axis_size(axis)
    return lax.ppermute(value, axis, [(i, (i + by) % devices) for i in range(devices)])


def attend_block(partial_state, query_part, key_part, value_part, visible):
    largest, denominator, numerator = partial_state
    scores = jnp.einsum("qkgd,skd->kgqs", query_part, key_part, preferred_element_type=jnp.float32)
    scores = scores * query_part.shape[-1] ** (-0.5)
    if visible is not None:
        scores = jnp.where(visible[None, None], scores, -jnp.inf)
    new_max = jnp.maximum(largest, jnp.max(scores, axis=-1))
    factor = jnp.exp(largest - new_max)
    exp_scores = jnp.exp(scores - new_max[..., None])
    denominator = denominator * factor + jnp.sum(exp_scores, axis=-1)
    weighted = jnp.einsum(
        "kgqs,skd->kgqd",
        exp_scores.astype(jnp.bfloat16),
        value_part,
        preferred_element_type=jnp.float32,
    )
    return (new_max, denominator, numerator * factor[..., None] + weighted)


def update_half(partial_state, grouped, offset, key_part, value_part):
    span_rows = key_part.shape[0]
    sliced = tuple(
        (lax.dynamic_slice_in_dim(member, offset, span_rows, 2) for member in partial_state)
    )
    query_part = lax.dynamic_slice_in_dim(grouped, offset, span_rows, 0)
    renewed = attend_block(sliced, query_part, key_part, value_part, None)
    return tuple(
        (
            lax.dynamic_update_slice_in_dim(member, updated, offset, 2)
            for member, updated in zip(partial_state, renewed)
        )
    )


def remote_step(partial_state, grouped, own_first, arrived):
    key_part, value_part, key_places = arrived
    half_rows = key_part.shape[0] // 2
    partial_state = update_half(
        partial_state, grouped, half_rows, key_part[:half_rows], value_part[:half_rows]
    )
    offset = jnp.where(key_places[0] < own_first, 0, half_rows).astype(jnp.int32)
    key_pick = lax.dynamic_slice_in_dim(key_part, offset, half_rows, 0)
    value_pick = lax.dynamic_slice_in_dim(value_part, offset, half_rows, 0)
    return update_half(partial_state, grouped, offset, key_pick, value_pick)


def local(query_states, key_states, value_rows, positions, out_weight):
    tokens, query_heads, head_size = query_states.shape
    kv_heads = key_states.shape[1]
    grouped = query_states.reshape(tokens, kv_heads, query_heads // kv_heads, head_size)
    row_shape = (kv_heads, query_heads // kv_heads, tokens)
    partial_state = (
        jnp.full(row_shape, LOW_START, jnp.float32),
        jnp.zeros(row_shape, jnp.float32),
        jnp.zeros(row_shape + (head_size,), jnp.float32),
    )
    visible = positions[None, :] <= positions[:, None]
    partial_state = attend_block(partial_state, grouped, key_states, value_rows, visible)
    own_first = positions[0]
    own_block = (key_states, value_rows, positions)

    def paired_turn(number, status):
        forward_block = from_behind(for_sending(status[0]), "ctx", 1)
        backward_block = from_behind(for_sending(status[1]), "ctx", -1)
        updated = remote_step(status[2], grouped, own_first, forward_block)
        return (
            forward_block,
            backward_block,
            remote_step(updated, grouped, own_first, backward_block),
        )

    forward_block, backward_block, partial_state = lax.fori_loop(
        0, lax.axis_size("ctx") // 2 - 1, paired_turn, (own_block, own_block, partial_state)
    )
    forward_block = from_behind((forward_block[0], forward_block[1], forward_block[2]), "ctx", 1)
    partial_state = remote_step(partial_state, grouped, own_first, forward_block)
    largest, denominator, numerator = partial_state
    attended = numerator / denominator[..., None]
    attended = (
        jnp.transpose(attended, (2, 0, 1, 3))
        .reshape(tokens, query_heads * head_size)
        .astype(jnp.bfloat16)
    )
    combined = jnp.dot(
        attended,
        lax.all_gather(out_weight, "ctx", axis=1, tiled=True),
        preferred_element_type=jnp.float32,
    )
    return lax.psum_scatter(combined.astype(jnp.bfloat16), "tp", scatter_dimension=1, tiled=True)


def solution(mesh):
    in_specs = (
        P(("groups", "ctx"), "tp", None),
        P(("groups", "ctx"), "tp", None),
        P(("groups", "ctx"), "tp", None),
        P(("groups", "ctx")),
        P("tp", "ctx"),
    )
    out_specs = P(("groups", "ctx"), "tp")
    return jax.shard_map(local, mesh=mesh, in_specs=in_specs, out_specs=out_specs, check_vma=False)
```

profile of v0, /device:TPU:24, one launch (start us, length us, event | category | flops | bytes accessed | tf_op | source)
XLA Modules:
  0.0 304.5 jit_solution(16541686497031300502)
XLA Ops:
  7.8 2.5 copy.10
  11.0 1.7 copy.71
  14.8 1.8 fusion.53
  16.6 4.5 %broadcast_add_fusion = f32[4,8,256,128]{3,2,1,0:T(8,128)} fusion(f32[4,8,256]{2,1,0:T(8,128)S(1)} %get-tuple-element.146, f32[4,256,256,8]{2,1,3,0:T(8,128)S(1)} %get-tuple-element.149, f32[4,8,256]{2,1,0:T(8,128)S(1)} %broadcast_maximum_fusion, pred[256,256]{0,1:T(8,128)(4,1)S(1)} %broadcast_compare_fusion, bf16[256,4,128,1]{2,1,0,3:T(4,128)(2,1)S(1)} %bitcast.207), kind=kOutput, calls=%fused_computation.102 | convolution fusion | flops 546308096 | bytes 12976128 | tf_op jit(solution)/shard_map/kgqs,skd->kgqd/dot_general | solution.py:28
  21.1 235.7 %while.26 = (s32[]{:T(128)}, bf16[256,4,128]{2,0,1:T(8,128)(2,1)}, bf16[256,4,128]{2,0,1:T(8,128)(2,1)S(1)}, s32[256]{0:T(256)S(1)}, bf16[256,4,128]{2,0,1:T(8,1...) while((s32[]{:T(128)}, bf16[256,4,128]{2,0,1:T(8,128)(2,1)}, ...), condition=%wide.region_11.12_spmd, body=%wide.region_2.11_spmd.sunk | while | flops 1094746112 | bytes 88293880 | solution.py:89
  23.8 2.6 collective-permute-start.3
  26.4 7.4 %collective-permute-done.2 = s32[256]{0:T(256)S(1)} collective-permute-done((s32[256]{0:T(256)S(1)}, s32[256]{0:T(256)S(1)}, u32[]{:S(2)}, u32[]{:S(2)}) %collective-permute-start.2) | collective-permute-done | bytes 1056 | tf_op jit(solution)/shard_map/while/body/eval_jaxpr/ppermute | solution.py:15
  42.5 2.0 collective-permute-done.4
  50.6 2.0 copy-done.1
  52.7 5.3 %collective-permute-start = (bf16[256,4,128]{2,0,1:T(8,128)(2,1)}, bf16[256,4,128]{2,0,1:T(8,128)(2,1)S(1)}, u32[]{:S(2)}, u32[]{:S(2)}) collective-permute-start(bf16[256,4,128]{2,0,1:T(8,128)(2,1)} %get-tuple-element.291), channel_id=1, source_target_pairs={{0,1},{1,2},{2,3},{3,4},{4,5},{5,6},{6,7},{7,8},{8,9},{9,10},{10,1... | collective-permute-start | bytes 786440 | tf_op jit(solution)/shard_map/while/body/eval_jaxpr/ppermute | solution.py:15
  58.0 2.6 collective-permute-start.5
  60.7 2.6 collective-permute-start.3
  63.3 2.2 collective-permute-done.2
  71.0 2.3 collective-permute-done.3
  76.5 4.1 %collective-permute-done.4 = bf16[256,4,128]{2,0,1:T(8,128)(2,1)S(1)} collective-permute-done((bf16[256,4,128]{2,0,1:T(8,128)(2,1)}, bf16[256,4,128]{2,0,1:T(8,128)(2,1)S(1)}, u32[]{:S(2)}, u32[]{:S(2)}) %collective-permute-start.4) | collective-permute-done | bytes 262176 | tf_op jit(solution)/shard_map/while/body/eval_jaxpr/ppermute | solution.py:15
  86.7 2.2 copy-done.1
  88.8 3.2 %collective-permute-start = (bf16[256,4,128]{2,0,1:T(8,128)(2,1)}, bf16[256,4,128]{2,0,1:T(8,128)(2,1)S(1)}, u32[]{:S(2)}, u32[]{:S(2)}) collective-permute-start(bf16[256,4,128]{2,0,1:T(8,128)(2,1)} %get-tuple-element.291), channel_id=1, source_target_pairs={{0,1},{1,2},{2,3},{3,4},{4,5},{5,6},{6,7},{7,8},{8,9},{9,10},{10,1... | collective-permute-start | bytes 786440 | tf_op jit(solution)/shard_map/while/body/eval_jaxpr/ppermute | solution.py:15
  92.1 2.6 collective-permute-start.5
  94.7 2.6 collective-permute-start.3
  97.4 3.8 %collective-permute-done.2 = s32[256]{0:T(256)S(1)} collective-permute-done((s32[256]{0:T(256)S(1)}, s32[256]{0:T(256)S(1)}, u32[]{:S(2)}, u32[]{:S(2)}) %collective-permute-start.2) | collective-permute-done | bytes 1056 | tf_op jit(solution)/shard_map/while/body/eval_jaxpr/ppermute | solution.py:15
  110.6 3.9 %collective-permute-done.4 = bf16[256,4,128]{2,0,1:T(8,128)(2,1)S(1)} collective-permute-done((bf16[256,4,128]{2,0,1:T(8,128)(2,1)}, bf16[256,4,128]{2,0,1:T(8,128)(2,1)S(1)}, u32[]{:S(2)}, u32[]{:S(2)}) %collective-permute-start.4) | collective-permute-done | bytes 262176 | tf_op jit(solution)/shard_map/while/body/eval_jaxpr/ppermute | solution.py:15
  120.6 2.1 copy-done.1
  122.7 4.1 %collective-permute-start = (bf16[256,4,128]{2,0,1:T(8,128)(2,1)}, bf16[256,4,128]{2,0,1:T(8,128)(2,1)S(1)}, u32[]{:S(2)}, u32[]{:S(2)}) collective-permute-start(bf16[256,4,128]{2,0,1:T(8,128)(2,1)} %get-tuple-element.291), channel_id=1, source_target_pairs={{0,1},{1,2},{2,3},{3,4},{4,5},{5,6},{6,7},{7,8},{8,9},{9,10},{10,1... | collective-permute-start | bytes 786440 | tf_op jit(solution)/shard_map/while/body/eval_jaxpr/ppermute | solution.py:15
  126.8 2.6 collective-permute-start.5
  129.4 2.6 collective-permute-start.3
  132.1 2.7 collective-permute-done.2
  140.3 1.8 collective-permute-done.3
  145.3 2.9 collective-permute-done.4
  154.3 2.1 copy-done.1
  156.4 5.2 %collective-permute-start = (bf16[256,4,128]{2,0,1:T(8,128)(2,1)}, bf16[256,4,128]{2,0,1:T(8,128)(2,1)S(1)}, u32[]{:S(2)}, u32[]{:S(2)}) collective-permute-start(bf16[256,4,128]{2,0,1:T(8,128)(2,1)} %get-tuple-element.291), channel_id=1, source_target_pairs={{0,1},{1,2},{2,3},{3,4},{4,5},{5,6},{6,7},{7,8},{8,9},{9,10},{10,1... | collective-permute-start | bytes 786440 | tf_op jit(solution)/shard_map/while/body/eval_jaxpr/ppermute | solution.py:15
  161.6 2.6 collective-permute-start.5
  164.3 2.6 collective-permute-start.3
  174.0 2.8 collective-permute-done.3
  187.9 2.1 copy-done.1
  189.9 6.2 %collective-permute-start = (bf16[256,4,128]{2,0,1:T(8,128)(2,1)}, bf16[256,4,128]{2,0,1:T(8,128)(2,1)S(1)}, u32[]{:S(2)}, u32[]{:S(2)}) collective-permute-start(bf16[256,4,128]{2,0,1:T(8,128)(2,1)} %get-tuple-element.291), channel_id=1, source_target_pairs={{0,1},{1,2},{2,3},{3,4},{4,5},{5,6},{6,7},{7,8},{8,9},{9,10},{10,1... | collective-permute-start | bytes 786440 | tf_op jit(solution)/shard_map/while/body/eval_jaxpr/ppermute | solution.py:15
  196.1 2.6 collective-permute-start.5
  198.7 2.6 collective-permute-start.3
  207.6 3.3 %collective-permute-done.3 = bf16[256,4,128]{2,0,1:T(8,128)(2,1)S(1)} collective-permute-done((bf16[256,4,128]{2,0,1:T(8,128)(2,1)}, bf16[256,4,128]{2,0,1:T(8,128)(2,1)S(1)}, u32[]{:S(2)}, u32[]{:S(2)}) %collective-permute-start.3) | collective-permute-done | bytes 262176 | tf_op jit(solution)/shard_map/while/body/eval_jaxpr/ppermute | solution.py:15
  221.2 2.2 copy-done.1
  223.4 6.7 %collective-permute-start = (bf16[256,4,128]{2,0,1:T(8,128)(2,1)}, bf16[256,4,128]{2,0,1:T(8,128)(2,1)S(1)}, u32[]{:S(2)}, u32[]{:S(2)}) collective-permute-start(bf16[256,4,128]{2,0,1:T(8,128)(2,1)} %get-tuple-element.291), channel_id=1, source_target_pairs={{0,1},{1,2},{2,3},{3,4},{4,5},{5,6},{6,7},{7,8},{8,9},{9,10},{10,1... | collective-permute-start | bytes 786440 | tf_op jit(solution)/shard_map/while/body/eval_jaxpr/ppermute | solution.py:15
  230.1 2.6 collective-permute-start.5
  232.8 2.6 collective-permute-start.3
  240.9 3.9 %collective-permute-done.3 = bf16[256,4,128]{2,0,1:T(8,128)(2,1)S(1)} collective-permute-done((bf16[256,4,128]{2,0,1:T(8,128)(2,1)}, bf16[256,4,128]{2,0,1:T(8,128)(2,1)S(1)}, u32[]{:S(2)}, u32[]{:S(2)}) %collective-permute-start.3) | collective-permute-done | bytes 262176 | tf_op jit(solution)/shard_map/while/body/eval_jaxpr/ppermute | solution.py:15
  254.8 2.0 copy-done.1
  256.9 5.6 %collective-permute-start.6 = (bf16[256,4,128]{2,0,1:T(8,128)(2,1)}, bf16[256,4,128]{2,0,1:T(8,128)(2,1)}, u32[]{:S(2)}, u32[]{:S(2)}) collective-permute-start(bf16[256,4,128]{2,0,1:T(8,128)(2,1)} %get-tuple-element.74), channel_id=1, source_target_pairs={{0,1},{1,2},{2,3},{3,4},{4,5},{5,6},{6,7},{7,8},{8,9},{9,10},{10,1... | collective-permute-start | bytes 786440 | tf_op jit(solution)/shard_map/ppermute | solution.py:15
  262.4 1.8 collective-permute-start.8
  266.4 5.4 %copy.22 = f32[4,8,256,128]{2,3,1,0:T(8,128)} copy(f32[4,8,256,128]{3,2,1,0:T(8,128)} %get-tuple-element.72) | data formatting | bytes 8388608 | tf_op jit(solution)/shard_map/while | solution.py:89
  281.0 16.7 %convolution_convert_fusion = bf16[256,4096]{1,0:T(8,128)(2,1)} fusion(bf16[256,4096]{0,1:T(8,128)(2,1)S(1)} %bitcast.204, bf16[4096,4096]{1,0:T(8,128)(2,1)} %all-gather.2.cloned.1.call-done), kind=kOutput, calls=%fused_computation.85 | convolution fusion | flops 8590983168 | bytes 37748736 | tf_op jit(solution)/shard_map/dot_general | solution.py:101
  (332 shorter events, 108.1 us)
Async XLA Ops:
  6.5 274.4 %all-gather.2.cloned.1.call-start = ((), (), s32[]{:S(2)}) async-start(), calls=%async_computation | async-start | bytes 35651584 | tf_op jit(solution)/shard_map/all_gather | solution.py:103
  21.1 16.4 %collective-permute-start = (bf16[256,4,128]{2,0,1:T(8,128)(2,1)}, bf16[256,4,128]{2,0,1:T(8,128)(2,1)S(1)}, u32[]{:S(2)}, u32[]{:S(2)}) collective-permute-start(bf16[256,4,128]{2,0,1:T(8,128)(2,1)} %get-tuple-element.291), channel_id=1, source_target_pairs={{0,1},{1,2},{2,3},{3,4},{4,5},{5,6},{6,7},{7,8},{8,9},{9,10},{10,1... | collective-permute-start | bytes 786440 | tf_op jit(solution)/shard_map/while/body/eval_jaxpr/ppermute | solution.py:15
  21.1 12.7 %collective-permute-start.2 = (s32[256]{0:T(256)S(1)}, s32[256]{0:T(256)S(1)}, u32[]{:S(2)}, u32[]{:S(2)}) collective-permute-start(s32[256]{0:T(256)S(1)} %get-tuple-element.293), channel_id=1, source_target_pairs={{0,1},{1,2},{2,3},{3,4},{4,5},{5,6},{6,7},{7,8},{8,9},{9,10},{10,1... | collective-permute-start | bytes 3080 | tf_op jit(solution)/shard_map/while/body/eval_jaxpr/ppermute | solution.py:15
  22.7 12.9 %collective-permute-start.5 = (s32[256]{0:T(256)S(1)}, s32[256]{0:T(256)S(1)}, u32[]{:S(2)}, u32[]{:S(2)}) collective-permute-start(s32[256]{0:T(256)S(1)} %get-tuple-element.296), channel_id=1, source_target_pairs={{0,15},{1,0},{2,1},{3,2},{4,3},{5,4},{6,5},{7,6},{8,7},{9,8},{10,9... | collective-permute-start | bytes 3080 | tf_op jit(solution)/shard_map/while/body/eval_jaxpr/ppermute | solution.py:15
  23.8 18.7 %collective-permute-start.1 = (bf16[256,4,128]{2,0,1:T(8,128)(2,1)S(1)}, bf16[256,4,128]{2,0,1:T(8,128)(2,1)S(1)}, u32[]{:S(2)}, u32[]{:S(2)}) collective-permute-start(bf16[256,4,128]{2,0,1:T(8,128)(2,1)S(1)} %get-tuple-element.292), channel_id=1, source_target_pairs={{0,1},{1,2},{2,3},{3,4},{4,5},{5,6},{6,7},{7,8},{8,9},{9,10},{10,1... | collective-permute-start | bytes 786440 | tf_op jit(solution)/shard_map/while/body/eval_jaxpr/ppermute | solution.py:15
  23.8 15.5 %collective-permute-start.3 = (bf16[256,4,128]{2,0,1:T(8,128)(2,1)}, bf16[256,4,128]{2,0,1:T(8,128)(2,1)S(1)}, u32[]{:S(2)}, u32[]{:S(2)}) collective-permute-start(bf16[256,4,128]{2,0,1:T(8,128)(2,1)} %get-tuple-element.294), channel_id=1, source_target_pairs={{0,15},{1,0},{2,1},{3,2},{4,3},{5,4},{6,5},{7,6},{8,7},{9,8},{10,9... | collective-permute-start | bytes 786440 | tf_op jit(solution)/shard_map/while/body/eval_jaxpr/ppermute | solution.py:15
  33.8 10.7 %collective-permute-start.4 = (bf16[256,4,128]{2,0,1:T(8,128)(2,1)}, bf16[256,4,128]{2,0,1:T(8,128)(2,1)S(1)}, u32[]{:S(2)}, u32[]{:S(2)}) collective-permute-start(bf16[256,4,128]{2,0,1:T(8,128)(2,1)} %get-tuple-element.295), channel_id=1, source_target_pairs={{0,15},{1,0},{2,1},{3,2},{4,3},{5,4},{6,5},{7,6},{8,7},{9,8},{10,9... | collective-permute-start | bytes 786440 | tf_op jit(solution)/shard_map/while/body/eval_jaxpr/ppermute | solution.py:15
  52.7 16.5 %collective-permute-start = (bf16[256,4,128]{2,0,1:T(8,128)(2,1)}, bf16[256,4,128]{2,0,1:T(8,128)(2,1)S(1)}, u32[]{:S(2)}, u32[]{:S(2)}) collective-permute-start(bf16[256,4,128]{2,0,1:T(8,128)(2,1)} %get-tuple-element.291), channel_id=1, source_target_pairs={{0,1},{1,2},{2,3},{3,4},{4,5},{5,6},{6,7},{7,8},{8,9},{9,10},{10,1... | collective-permute-start | bytes 786440 | tf_op jit(solution)/shard_map/while/body/eval_jaxpr/ppermute | solution.py:15
  58.0 7.5 %collective-permute-start.2 = (s32[256]{0:T(256)S(1)}, s32[256]{0:T(256)S(1)}, u32[]{:S(2)}, u32[]{:S(2)}) collective-permute-start(s32[256]{0:T(256)S(1)} %get-tuple-element.293), channel_id=1, source_target_pairs={{0,1},{1,2},{2,3},{3,4},{4,5},{5,6},{6,7},{7,8},{8,9},{9,10},{10,1... | collective-permute-start | bytes 3080 | tf_op jit(solution)/shard_map/while/body/eval_jaxpr/ppermute | solution.py:15
  58.0 9.3 %collective-permute-start.5 = (s32[256]{0:T(256)S(1)}, s32[256]{0:T(256)S(1)}, u32[]{:S(2)}, u32[]{:S(2)}) collective-permute-start(s32[256]{0:T(256)S(1)} %get-tuple-element.296), channel_id=1, source_target_pairs={{0,15},{1,0},{2,1},{3,2},{4,3},{5,4},{6,5},{7,6},{8,7},{9,8},{10,9... | collective-permute-start | bytes 3080 | tf_op jit(solution)/shard_map/while/body/eval_jaxpr/ppermute | solution.py:15
  60.7 15.8 %collective-permute-start.1 = (bf16[256,4,128]{2,0,1:T(8,128)(2,1)S(1)}, bf16[256,4,128]{2,0,1:T(8,128)(2,1)S(1)}, u32[]{:S(2)}, u32[]{:S(2)}) collective-permute-start(bf16[256,4,128]{2,0,1:T(8,128)(2,1)S(1)} %get-tuple-element.292), channel_id=1, source_target_pairs={{0,1},{1,2},{2,3},{3,4},{4,5},{5,6},{6,7},{7,8},{8,9},{9,10},{10,1... | collective-permute-start | bytes 786440 | tf_op jit(solution)/shard_map/while/body/eval_jaxpr/ppermute | solution.py:15
  60.7 12.6 %collective-permute-start.3 = (bf16[256,4,128]{2,0,1:T(8,128)(2,1)}, bf16[256,4,128]{2,0,1:T(8,128)(2,1)S(1)}, u32[]{:S(2)}, u32[]{:S(2)}) collective-permute-start(bf16[256,4,128]{2,0,1:T(8,128)(2,1)} %get-tuple-element.294), channel_id=1, source_target_pairs={{0,15},{1,0},{2,1},{3,2},{4,3},{5,4},{6,5},{7,6},{8,7},{9,8},{10,9... | collective-permute-start | bytes 786440 | tf_op jit(solution)/shard_map/while/body/eval_jaxpr/ppermute | solution.py:15
  65.5 15.0 %collective-permute-start.4 = (bf16[256,4,128]{2,0,1:T(8,128)(2,1)}, bf16[256,4,128]{2,0,1:T(8,128)(2,1)S(1)}, u32[]{:S(2)}, u32[]{:S(2)}) collective-permute-start(bf16[256,4,128]{2,0,1:T(8,128)(2,1)} %get-tuple-element.295), channel_id=1, source_target_pairs={{0,15},{1,0},{2,1},{3,2},{4,3},{5,4},{6,5},{7,6},{8,7},{9,8},{10,9... | collective-permute-start | bytes 786440 | tf_op jit(solution)/shard_map/while/body/eval_jaxpr/ppermute | solution.py:15
  74.6 6.6 %copy-start = (f32[4,8,256,128]{3,2,1,0:T(8,128)S(1)}, f32[4,8,256,128]{3,2,1,0:T(8,128)}, u32[]{:S(2)}) copy-start(f32[4,8,256,128]{3,2,1,0:T(8,128)} %get-tuple-element.299) | copy-start | bytes 12582916 | tf_op jit(solution)/shard_map/while
  88.8 15.9 %collective-permute-start = (bf16[256,4,128]{2,0,1:T(8,128)(2,1)}, bf16[256,4,128]{2,0,1:T(8,128)(2,1)S(1)}, u32[]{:S(2)}, u32[]{:S(2)}) collective-permute-start(bf16[256,4,128]{2,0,1:T(8,128)(2,1)} %get-tuple-element.291), channel_id=1, source_target_pairs={{0,1},{1,2},{2,3},{3,4},{4,5},{5,6},{6,7},{7,8},{8,9},{9,10},{10,1... | collective-permute-start | bytes 786440 | tf_op jit(solution)/shard_map/while/body/eval_jaxpr/ppermute | solution.py:15
  92.1 9.1 %collective-permute-start.2 = (s32[256]{0:T(256)S(1)}, s32[256]{0:T(256)S(1)}, u32[]{:S(2)}, u32[]{:S(2)}) collective-permute-start(s32[256]{0:T(256)S(1)} %get-tuple-element.293), channel_id=1, source_target_pairs={{0,1},{1,2},{2,3},{3,4},{4,5},{5,6},{6,7},{7,8},{8,9},{9,10},{10,1... | collective-permute-start | bytes 3080 | tf_op jit(solution)/shard_map/while/body/eval_jaxpr/ppermute | solution.py:15
  92.1 10.9 %collective-permute-start.5 = (s32[256]{0:T(256)S(1)}, s32[256]{0:T(256)S(1)}, u32[]{:S(2)}, u32[]{:S(2)}) collective-permute-start(s32[256]{0:T(256)S(1)} %get-tuple-element.296), channel_id=1, source_target_pairs={{0,15},{1,0},{2,1},{3,2},{4,3},{5,4},{6,5},{7,6},{8,7},{9,8},{10,9... | collective-permute-start | bytes 3080 | tf_op jit(solution)/shard_map/while/body/eval_jaxpr/ppermute | solution.py:15
  94.7 15.8 %collective-permute-start.1 = (bf16[256,4,128]{2,0,1:T(8,128)(2,1)S(1)}, bf16[256,4,128]{2,0,1:T(8,128)(2,1)S(1)}, u32[]{:S(2)}, u32[]{:S(2)}) collective-permute-start(bf16[256,4,128]{2,0,1:T(8,128)(2,1)S(1)} %get-tuple-element.292), channel_id=1, source_target_pairs={{0,1},{1,2},{2,3},{3,4},{4,5},{5,6},{6,7},{7,8},{8,9},{9,10},{10,1... | collective-permute-start | bytes 786440 | tf_op jit(solution)/shard_map/while/body/eval_jaxpr/ppermute | solution.py:15
  94.7 12.6 %collective-permute-start.3 = (bf16[256,4,128]{2,0,1:T(8,128)(2,1)}, bf16[256,4,128]{2,0,1:T(8,128)(2,1)S(1)}, u32[]{:S(2)}, u32[]{:S(2)}) collective-permute-start(bf16[256,4,128]{2,0,1:T(8,128)(2,1)} %get-tuple-element.294), channel_id=1, source_target_pairs={{0,15},{1,0},{2,1},{3,2},{4,3},{5,4},{6,5},{7,6},{8,7},{9,8},{10,9... | collective-permute-start | bytes 786440 | tf_op jit(solution)/shard_map/while/body/eval_jaxpr/ppermute | solution.py:15
  101.1 13.3 %collective-permute-start.4 = (bf16[256,4,128]{2,0,1:T(8,128)(2,1)}, bf16[256,4,128]{2,0,1:T(8,128)(2,1)S(1)}, u32[]{:S(2)}, u32[]{:S(2)}) collective-permute-start(bf16[256,4,128]{2,0,1:T(8,128)(2,1)} %get-tuple-element.295), channel_id=1, source_target_pairs={{0,15},{1,0},{2,1},{3,2},{4,3},{5,4},{6,5},{7,6},{8,7},{9,8},{10,9... | collective-permute-start | bytes 786440 | tf_op jit(solution)/shard_map/while/body/eval_jaxpr/ppermute | solution.py:15
  122.7 15.8 %collective-permute-start = (bf16[256,4,128]{2,0,1:T(8,128)(2,1)}, bf16[256,4,128]{2,0,1:T(8,128)(2,1)S(1)}, u32[]{:S(2)}, u32[]{:S(2)}) collective-permute-start(bf16[256,4,128]{2,0,1:T(8,128)(2,1)} %get-tuple-element.291), channel_id=1, source_target_pairs={{0,1},{1,2},{2,3},{3,4},{4,5},{5,6},{6,7},{7,8},{8,9},{9,10},{10,1... | collective-permute-start | bytes 786440 | tf_op jit(solution)/shard_map/while/body/eval_jaxpr/ppermute | solution.py:15
  126.8 8.0 %collective-permute-start.2 = (s32[256]{0:T(256)S(1)}, s32[256]{0:T(256)S(1)}, u32[]{:S(2)}, u32[]{:S(2)}) collective-permute-start(s32[256]{0:T(256)S(1)} %get-tuple-element.293), channel_id=1, source_target_pairs={{0,1},{1,2},{2,3},{3,4},{4,5},{5,6},{6,7},{7,8},{8,9},{9,10},{10,1... | collective-permute-start | bytes 3080 | tf_op jit(solution)/shard_map/while/body/eval_jaxpr/ppermute | solution.py:15
  126.8 9.8 %collective-permute-start.5 = (s32[256]{0:T(256)S(1)}, s32[256]{0:T(256)S(1)}, u32[]{:S(2)}, u32[]{:S(2)}) collective-permute-start(s32[256]{0:T(256)S(1)} %get-tuple-element.296), channel_id=1, source_target_pairs={{0,15},{1,0},{2,1},{3,2},{4,3},{5,4},{6,5},{7,6},{8,7},{9,8},{10,9... | collective-permute-start | bytes 3080 | tf_op jit(solution)/shard_map/while/body/eval_jaxpr/ppermute | solution.py:15
  129.4 15.8 %collective-permute-start.1 = (bf16[256,4,128]{2,0,1:T(8,128)(2,1)S(1)}, bf16[256,4,128]{2,0,1:T(8,128)(2,1)S(1)}, u32[]{:S(2)}, u32[]{:S(2)}) collective-permute-start(bf16[256,4,128]{2,0,1:T(8,128)(2,1)S(1)} %get-tuple-element.292), channel_id=1, source_target_pairs={{0,1},{1,2},{2,3},{3,4},{4,5},{5,6},{6,7},{7,8},{8,9},{9,10},{10,1... | collective-permute-start | bytes 786440 | tf_op jit(solution)/shard_map/while/body/eval_jaxpr/ppermute | solution.py:15
  129.4 12.6 %collective-permute-start.3 = (bf16[256,4,128]{2,0,1:T(8,128)(2,1)}, bf16[256,4,128]{2,0,1:T(8,128)(2,1)S(1)}, u32[]{:S(2)}, u32[]{:S(2)}) collective-permute-start(bf16[256,4,128]{2,0,1:T(8,128)(2,1)} %get-tuple-element.294), channel_id=1, source_target_pairs={{0,15},{1,0},{2,1},{3,2},{4,3},{5,4},{6,5},{7,6},{8,7},{9,8},{10,9... | collective-permute-start | bytes 786440 | tf_op jit(solution)/shard_map/while/body/eval_jaxpr/ppermute | solution.py:15
  134.8 13.4 %collective-permute-start.4 = (bf16[256,4,128]{2,0,1:T(8,128)(2,1)}, bf16[256,4,128]{2,0,1:T(8,128)(2,1)S(1)}, u32[]{:S(2)}, u32[]{:S(2)}) collective-permute-start(bf16[256,4,128]{2,0,1:T(8,128)(2,1)} %get-tuple-element.295), channel_id=1, source_target_pairs={{0,15},{1,0},{2,1},{3,2},{4,3},{5,4},{6,5},{7,6},{8,7},{9,8},{10,9... | collective-permute-start | bytes 786440 | tf_op jit(solution)/shard_map/while/body/eval_jaxpr/ppermute | solution.py:15
  156.4 15.8 %collective-permute-start = (bf16[256,4,128]{2,0,1:T(8,128)(2,1)}, bf16[256,4,128]{2,0,1:T(8,128)(2,1)S(1)}, u32[]{:S(2)}, u32[]{:S(2)}) collective-permute-start(bf16[256,4,128]{2,0,1:T(8,128)(2,1)} %get-tuple-element.291), channel_id=1, source_target_pairs={{0,1},{1,2},{2,3},{3,4},{4,5},{5,6},{6,7},{7,8},{8,9},{9,10},{10,1... | collective-permute-start | bytes 786440 | tf_op jit(solution)/shard_map/while/body/eval_jaxpr/ppermute | solution.py:15
  161.6 7.0 %collective-permute-start.2 = (s32[256]{0:T(256)S(1)}, s32[256]{0:T(256)S(1)}, u32[]{:S(2)}, u32[]{:S(2)}) collective-permute-start(s32[256]{0:T(256)S(1)} %get-tuple-element.293), channel_id=1, source_target_pairs={{0,1},{1,2},{2,3},{3,4},{4,5},{5,6},{6,7},{7,8},{8,9},{9,10},{10,1... | collective-permute-start | bytes 3080 | tf_op jit(solution)/shard_map/while/body/eval_jaxpr/ppermute | solution.py:15
  161.6 8.8 %collective-permute-start.5 = (s32[256]{0:T(256)S(1)}, s32[256]{0:T(256)S(1)}, u32[]{:S(2)}, u32[]{:S(2)}) collective-permute-start(s32[256]{0:T(256)S(1)} %get-tuple-element.296), channel_id=1, source_target_pairs={{0,15},{1,0},{2,1},{3,2},{4,3},{5,4},{6,5},{7,6},{8,7},{9,8},{10,9... | collective-permute-start | bytes 3080 | tf_op jit(solution)/shard_map/while/body/eval_jaxpr/ppermute | solution.py:15
  164.3 15.8 %collective-permute-start.1 = (bf16[256,4,128]{2,0,1:T(8,128)(2,1)S(1)}, bf16[256,4,128]{2,0,1:T(8,128)(2,1)S(1)}, u32[]{:S(2)}, u32[]{:S(2)}) collective-permute-start(bf16[256,4,128]{2,0,1:T(8,128)(2,1)S(1)} %get-tuple-element.292), channel_id=1, source_target_pairs={{0,1},{1,2},{2,3},{3,4},{4,5},{5,6},{6,7},{7,8},{8,9},{9,10},{10,1... | collective-permute-start | bytes 786440 | tf_op jit(solution)/shard_map/while/body/eval_jaxpr/ppermute | solution.py:15
  164.3 12.6 %collective-permute-start.3 = (bf16[256,4,128]{2,0,1:T(8,128)(2,1)}, bf16[256,4,128]{2,0,1:T(8,128)(2,1)S(1)}, u32[]{:S(2)}, u32[]{:S(2)}) collective-permute-start(bf16[256,4,128]{2,0,1:T(8,128)(2,1)} %get-tuple-element.294), channel_id=1, source_target_pairs={{0,15},{1,0},{2,1},{3,2},{4,3},{5,4},{6,5},{7,6},{8,7},{9,8},{10,9... | collective-permute-start | bytes 786440 | tf_op jit(solution)/shard_map/while/body/eval_jaxpr/ppermute | solution.py:15
  168.6 13.2 %collective-permute-start.4 = (bf16[256,4,128]{2,0,1:T(8,128)(2,1)}, bf16[256,4,128]{2,0,1:T(8,128)(2,1)S(1)}, u32[]{:S(2)}, u32[]{:S(2)}) collective-permute-start(bf16[256,4,128]{2,0,1:T(8,128)(2,1)} %get-tuple-element.295), channel_id=1, source_target_pairs={{0,15},{1,0},{2,1},{3,2},{4,3},{5,4},{6,5},{7,6},{8,7},{9,8},{10,9... | collective-permute-start | bytes 786440 | tf_op jit(solution)/shard_map/while/body/eval_jaxpr/ppermute | solution.py:15
  189.9 15.9 %collective-permute-start = (bf16[256,4,128]{2,0,1:T(8,128)(2,1)}, bf16[256,4,128]{2,0,1:T(8,128)(2,1)S(1)}, u32[]{:S(2)}, u32[]{:S(2)}) collective-permute-start(bf16[256,4,128]{2,0,1:T(8,128)(2,1)} %get-tuple-element.291), channel_id=1, source_target_pairs={{0,1},{1,2},{2,3},{3,4},{4,5},{5,6},{6,7},{7,8},{8,9},{9,10},{10,1... | collective-permute-start | bytes 786440 | tf_op jit(solution)/shard_map/while/body/eval_jaxpr/ppermute | solution.py:15
  196.1 6.1 %collective-permute-start.2 = (s32[256]{0:T(256)S(1)}, s32[256]{0:T(256)S(1)}, u32[]{:S(2)}, u32[]{:S(2)}) collective-permute-start(s32[256]{0:T(256)S(1)} %get-tuple-element.293), channel_id=1, source_target_pairs={{0,1},{1,2},{2,3},{3,4},{4,5},{5,6},{6,7},{7,8},{8,9},{9,10},{10,1... | collective-permute-start | bytes 3080 | tf_op jit(solution)/shard_map/while/body/eval_jaxpr/ppermute | solution.py:15
  196.1 7.9 %collective-permute-start.5 = (s32[256]{0:T(256)S(1)}, s32[256]{0:T(256)S(1)}, u32[]{:S(2)}, u32[]{:S(2)}) collective-permute-start(s32[256]{0:T(256)S(1)} %get-tuple-element.296), channel_id=1, source_target_pairs={{0,15},{1,0},{2,1},{3,2},{4,3},{5,4},{6,5},{7,6},{8,7},{9,8},{10,9... | collective-permute-start | bytes 3080 | tf_op jit(solution)/shard_map/while/body/eval_jaxpr/ppermute | solution.py:15
  198.7 15.5 %collective-permute-start.1 = (bf16[256,4,128]{2,0,1:T(8,128)(2,1)S(1)}, bf16[256,4,128]{2,0,1:T(8,128)(2,1)S(1)}, u32[]{:S(2)}, u32[]{:S(2)}) collective-permute-start(bf16[256,4,128]{2,0,1:T(8,128)(2,1)S(1)} %get-tuple-element.292), channel_id=1, source_target_pairs={{0,1},{1,2},{2,3},{3,4},{4,5},{5,6},{6,7},{7,8},{8,9},{9,10},{10,1... | collective-permute-start | bytes 786440 | tf_op jit(solution)/shard_map/while/body/eval_jaxpr/ppermute | solution.py:15
  198.7 12.3 %collective-permute-start.3 = (bf16[256,4,128]{2,0,1:T(8,128)(2,1)}, bf16[256,4,128]{2,0,1:T(8,128)(2,1)S(1)}, u32[]{:S(2)}, u32[]{:S(2)}) collective-permute-start(bf16[256,4,128]{2,0,1:T(8,128)(2,1)} %get-tuple-element.294), channel_id=1, source_target_pairs={{0,15},{1,0},{2,1},{3,2},{4,3},{5,4},{6,5},{7,6},{8,7},{9,8},{10,9... | collective-permute-start | bytes 786440 | tf_op jit(solution)/shard_map/while/body/eval_jaxpr/ppermute | solution.py:15
  202.2 12.9 %collective-permute-start.4 = (bf16[256,4,128]{2,0,1:T(8,128)(2,1)}, bf16[256,4,128]{2,0,1:T(8,128)(2,1)S(1)}, u32[]{:S(2)}, u32[]{:S(2)}) collective-permute-start(bf16[256,4,128]{2,0,1:T(8,128)(2,1)} %get-tuple-element.295), channel_id=1, source_target_pairs={{0,15},{1,0},{2,1},{3,2},{4,3},{5,4},{6,5},{7,6},{8,7},{9,8},{10,9... | collective-permute-start | bytes 786440 | tf_op jit(solution)/shard_map/while/body/eval_jaxpr/ppermute | solution.py:15
  223.4 15.7 %collective-permute-start = (bf16[256,4,128]{2,0,1:T(8,128)(2,1)}, bf16[256,4,128]{2,0,1:T(8,128)(2,1)S(1)}, u32[]{:S(2)}, u32[]{:S(2)}) collective-permute-start(bf16[256,4,128]{2,0,1:T(8,128)(2,1)} %get-tuple-element.291), channel_id=1, source_target_pairs={{0,1},{1,2},{2,3},{3,4},{4,5},{5,6},{6,7},{7,8},{8,9},{9,10},{10,1... | collective-permute-start | bytes 786440 | tf_op jit(solution)/shard_map/while/body/eval_jaxpr/ppermute | solution.py:15
  230.1 5.3 %collective-permute-start.2 = (s32[256]{0:T(256)S(1)}, s32[256]{0:T(256)S(1)}, u32[]{:S(2)}, u32[]{:S(2)}) collective-permute-start(s32[256]{0:T(256)S(1)} %get-tuple-element.293), channel_id=1, source_target_pairs={{0,1},{1,2},{2,3},{3,4},{4,5},{5,6},{6,7},{7,8},{8,9},{9,10},{10,1... | collective-permute-start | bytes 3080 | tf_op jit(solution)/shard_map/while/body/eval_jaxpr/ppermute | solution.py:15
  230.1 7.1 %collective-permute-start.5 = (s32[256]{0:T(256)S(1)}, s32[256]{0:T(256)S(1)}, u32[]{:S(2)}, u32[]{:S(2)}) collective-permute-start(s32[256]{0:T(256)S(1)} %get-tuple-element.296), channel_id=1, source_target_pairs={{0,15},{1,0},{2,1},{3,2},{4,3},{5,4},{6,5},{7,6},{8,7},{9,8},{10,9... | collective-permute-start | bytes 3080 | tf_op jit(solution)/shard_map/while/body/eval_jaxpr/ppermute | solution.py:15
  232.8 15.3 %collective-permute-start.1 = (bf16[256,4,128]{2,0,1:T(8,128)(2,1)S(1)}, bf16[256,4,128]{2,0,1:T(8,128)(2,1)S(1)}, u32[]{:S(2)}, u32[]{:S(2)}) collective-permute-start(bf16[256,4,128]{2,0,1:T(8,128)(2,1)S(1)} %get-tuple-element.292), channel_id=1, source_target_pairs={{0,1},{1,2},{2,3},{3,4},{4,5},{5,6},{6,7},{7,8},{8,9},{9,10},{10,1... | collective-permute-start | bytes 786440 | tf_op jit(solution)/shard_map/while/body/eval_jaxpr/ppermute | solution.py:15
  232.8 12.0 %collective-permute-start.3 = (bf16[256,4,128]{2,0,1:T(8,128)(2,1)}, bf16[256,4,128]{2,0,1:T(8,128)(2,1)S(1)}, u32[]{:S(2)}, u32[]{:S(2)}) collective-permute-start(bf16[256,4,128]{2,0,1:T(8,128)(2,1)} %get-tuple-element.294), channel_id=1, source_target_pairs={{0,15},{1,0},{2,1},{3,2},{4,3},{5,4},{6,5},{7,6},{8,7},{9,8},{10,9... | collective-permute-start | bytes 786440 | tf_op jit(solution)/shard_map/while/body/eval_jaxpr/ppermute | solution.py:15
  235.4 13.3 %collective-permute-start.4 = (bf16[256,4,128]{2,0,1:T(8,128)(2,1)}, bf16[256,4,128]{2,0,1:T(8,128)(2,1)S(1)}, u32[]{:S(2)}, u32[]{:S(2)}) collective-permute-start(bf16[256,4,128]{2,0,1:T(8,128)(2,1)} %get-tuple-element.295), channel_id=1, source_target_pairs={{0,15},{1,0},{2,1},{3,2},{4,3},{5,4},{6,5},{7,6},{8,7},{9,8},{10,9... | collective-permute-start | bytes 786440 | tf_op jit(solution)/shard_map/while/body/eval_jaxpr/ppermute | solution.py:15
  256.8 8.2 %slice-start = ((bf16[256,32,128]{2,1,0:T(8,128)(2,1)}), bf16[128,32,128]{2,1,0:T(8,128)(2,1)S(1)}, s32[]{:S(2)}) async-start(bf16[256,32,128]{2,1,0:T(8,128)(2,1)} %param.7), calls=%async_computation.1 | async-start | bytes 2097152 | tf_op jit(solution)/shard_map/dynamic_slice | solution.py:42
  256.9 16.8 %collective-permute-start.6 = (bf16[256,4,128]{2,0,1:T(8,128)(2,1)}, bf16[256,4,128]{2,0,1:T(8,128)(2,1)}, u32[]{:S(2)}, u32[]{:S(2)}) collective-permute-start(bf16[256,4,128]{2,0,1:T(8,128)(2,1)} %get-tuple-element.74), channel_id=1, source_target_pairs={{0,1},{1,2},{2,3},{3,4},{4,5},{5,6},{6,7},{7,8},{8,9},{9,10},{10,1... | collective-permute-start | bytes 786440 | tf_op jit(solution)/shard_map/ppermute | solution.py:15
  262.4 9.4 %collective-permute-start.8 = (s32[256]{0:T(256)S(1)}, s32[256]{0:T(256)S(1)}, u32[]{:S(2)}, u32[]{:S(2)}) collective-permute-start(s32[256]{0:T(256)S(1)} %get-tuple-element.76), channel_id=1, source_target_pairs={{0,1},{1,2},{2,3},{3,4},{4,5},{5,6},{6,7},{7,8},{8,9},{9,10},{10,1... | collective-permute-start | bytes 3080 | tf_op jit(solution)/shard_map/ppermute | solution.py:15
  265.0 12.3 %collective-permute-start.7 = (bf16[256,4,128]{0,2,1:T(8,128)(2,1)}, bf16[256,4,128]{0,2,1:T(8,128)(2,1)S(1)}, u32[]{:S(2)}, u32[]{:S(2)}) collective-permute-start(bf16[256,4,128]{0,2,1:T(8,128)(2,1)} %copy.20), channel_id=1, source_target_pairs={{0,1},{1,2},{2,3},{3,4},{4,5},{5,6},{6,7},{7,8},{8,9},{9,10},{10,1... | collective-permute-start | bytes 786440 | tf_op jit(solution)/shard_map/ppermute | solution.py:15
  (17 other events, 55.0 us)
Sparse Core Ops, SparseCore 0:
  8.8 249.2 all-gather.1
where the time goes:
time: 310 us; the launch traced here: 305 us
  matrix products  77 us (25%)
  starting transfers between devices  75.3 us (24%)
  local copies, waits for them, and re-layouts  53.5 us (17%)
  waiting for transfers between devices  49.6 us (16%)
  loops' own time  19 us (6%)
  other arithmetic  15.3 us (5%)
  between operations  14.9 us (5%)
    ppermute x45, starting transfers between devices, from_behind(): lax.ppermute(value, axis, [(i, (i + by) % devices) for i in range(devices)])  75.3 us
    ppermute x45, waiting for transfers between devices, from_behind(): lax.ppermute(value, axis, [(i, (i + by) % devices) for i in range(devices)])  49.6 us
    dot_general x31, matrix products, attend_block(): jnp.einsum('kgqs,skd->kgqd', exp_scores.astype(jnp.bfloat16), value_part,...  43.8 us
    while x98, local copies, waits for them, and re-layouts  29.7 us
    another operation x1, loops' own time, local(): lax.fori_loop(0, lax.axis_size('ctx') // 2 - 1, paired_turn, (own_block,...  19 us
    dot_general x1, matrix products, local(): jnp.dot(attended, lax.all_gather(out_weight, 'ctx', axis=1, tiled=True),...  16.7 us
    dot_general x31, matrix products, attend_block(): jnp.einsum('qkgd,skd->kgqs', query_part, key_part, preferred_element_type...  16.5 us
    reduce_sum x31, other arithmetic, attend_block(): denominator = denominator * factor + jnp.sum(exp_scores, axis=-1)  13.9 us
  transfers between devices with their start and end apart: 46, of which 19 were waited for; matrix products, arithmetic and copies ran while one was open for 37% of the time, Pallas kernels for 0%

commit v1 on v0

v1 whole, which is shorter than its diff:
```python
import functools
import math

import jax
import jax.numpy as jnp
from jax import lax
from jax.experimental import pallas as pl
from jax.experimental.pallas import tpu as pltpu
from jax.sharding import PartitionSpec as P

LOW_START = -1e30
BLOCKS_PER_STEP = 4
CHUNK = 256


def attend_kernel(half, group, place_ref, own_ref, q_ref, k_ref, v_ref, out_ref, acc_ref, max_ref, sum_ref):
    rows = group * half
    head_size = q_ref.shape[-1]
    span = BLOCKS_PER_STEP * half
    chunk = min(CHUNK, rows)
    to_exp2 = head_size ** (-0.5) * math.log2(math.e)

    def step(which, number, masked, query_block):
        keys, values = [], []
        for i in range(BLOCKS_PER_STEP):
            place = place_ref[number * BLOCKS_PER_STEP + i]
            keys.append(k_ref[pl.ds(pl.multiple_of(place * half, half), half), :])
            values.append(v_ref[pl.ds(pl.multiple_of(place * half, half), half), :])
        key_part = jnp.concatenate(keys, axis=0)
        value_part = jnp.concatenate(values, axis=0)
        if masked:
            key_place = number * span + lax.broadcasted_iota(jnp.int32, (span, chunk), 0)
            query_place = query_block * half + lax.broadcasted_iota(jnp.int32, (span, chunk), 1) % half
            visible = key_place <= query_place
        for c in range(rows // chunk):
            cols = pl.ds(c * chunk, chunk)
            scores = lax.dot_general(
                key_part,
                q_ref[0, which, cols, :],
                (((1,), (1,)), ((), ())),
                preferred_element_type=jnp.float32,
            )
            if masked:
                scores = jnp.where(visible, scores, LOW_START)
            old_max = max_ref[:, cols]
            new_max = jnp.maximum(old_max, jnp.max(scores, axis=0, keepdims=True))
            factor = jnp.exp2((old_max - new_max) * to_exp2)
            exp_scores = jnp.exp2((scores - new_max) * to_exp2)
            max_ref[:, cols] = new_max
            sum_ref[:, cols] = sum_ref[:, cols] * factor + jnp.sum(exp_scores, axis=0, keepdims=True)
            weighted = lax.dot_general(
                value_part,
                exp_scores.astype(jnp.bfloat16),
                (((0,), (0,)), ((), ())),
                preferred_element_type=jnp.float32,
            )
            acc_ref[:, cols] = acc_ref[:, cols] * factor + weighted

    for which in range(2):
        query_block = own_ref[which]
        steps = query_block // BLOCKS_PER_STEP
        max_ref[...] = jnp.full_like(max_ref, LOW_START)
        sum_ref[...] = jnp.zeros_like(sum_ref)
        acc_ref[...] = jnp.zeros_like(acc_ref)

        @pl.loop(0, steps)
        def _(number):
            step(which, number, False, query_block)

        step(which, steps, True, query_block)
        for g in range(group):
            cols = pl.ds(g * half, half)
            attended = acc_ref[:, cols] / sum_ref[:, cols]
            out_ref[pl.ds(g * head_size, head_size), pl.ds(which * half, half)] = attended.astype(jnp.bfloat16)


def attend(query_parts, gathered, place, own, first_head, all_heads):
    kv_heads, _, rows, head_size = query_parts.shape
    keys_total = gathered.shape[0]
    blocks = place.shape[0]
    half = keys_total // blocks
    group = rows // half
    flops = 4 * kv_heads * rows * head_size * half * (blocks + 1)
    return pl.pallas_call(
        functools.partial(attend_kernel, half, group),
        out_shape=jax.ShapeDtypeStruct((kv_heads * group * head_size, 2 * half), jnp.bfloat16),
        grid_spec=pltpu.PrefetchScalarGridSpec(
            num_scalar_prefetch=2,
            grid=(kv_heads,),
            in_specs=[
                pl.BlockSpec((1, 2, rows, head_size), lambda h, *_: (h, 0, 0, 0)),
                pl.BlockSpec((keys_total, head_size), lambda h, *_: (0, h + first_head)),
                pl.BlockSpec((keys_total, head_size), lambda h, *_: (0, h + first_head + all_heads)),
            ],
            out_specs=pl.BlockSpec((group * head_size, 2 * half), lambda h, *_: (h, 0)),
            scratch_shapes=[
                pltpu.VMEM((head_size, rows), jnp.float32),
                pltpu.VMEM((1, rows), jnp.float32),
                pltpu.VMEM((1, rows), jnp.float32),
            ],
        ),
        compiler_params=pltpu.CompilerParams(
            dimension_semantics=("arbitrary",), vmem_limit_bytes=40 * 1024 * 1024
        ),
        cost_estimate=pl.CostEstimate(
            flops=flops, bytes_accessed=2 * gathered.size, transcendentals=flops // (4 * head_size)
        ),
        name="attend",
    )(place, own, query_parts, gathered, gathered)


def spread_kernel(devices, own_ref, out_ref, far_send, far_recv, side_send, side_recv, pair_send, pair_recv, own_sem):
    me = lax.axis_index("ctx")
    outers = devices // 4
    outer, middle, inner = me // 4, (me // 2) % 2, me % 2

    def at(o, m, i):
        return (o * 2 + m) * 2 + i

    side = at(outer, 1 - middle, inner)
    pair = at(outer, middle, 1 - inner)
    far = [at((outer + k) % outers, middle, inner) for k in range(1, outers)]
    barrier = pltpu.get_barrier_semaphore()
    for other in far + [side, pair]:
        pl.semaphore_signal(barrier, inc=1, device_id={"ctx": other}, device_id_type=pl.DeviceIdType.MESH)
    pl.semaphore_wait(barrier, outers + 1)

    def send(source, slot, sends, recvs, number, target):
        return pltpu.make_async_remote_copy(
            src_ref=source,
            dst_ref=out_ref.at[slot],
            send_sem=sends.at[number],
            recv_sem=recvs.at[number],
            device_id={"ctx": target},
            device_id_type=pl.DeviceIdType.MESH,
        )

    own = pltpu.make_async_copy(own_ref, out_ref.at[me], own_sem)
    far_copies = [send(own_ref, me, far_send, far_recv, k, far[k]) for k in range(outers - 1)]
    for copy in far_copies:
        copy.start()
    side_copies = [send(own_ref, me, side_send, side_recv, 0, side)]
    pair_copies = [send(own_ref, me, pair_send, pair_recv, 0, pair)]
    side_copies[0].start()
    pair_copies[0].start()
    own.start()
    for k in range(outers - 1):
        far_copies[k].wait_recv()
        slot = at((outer + outers - 1 - k) % outers, middle, inner)
        side_copies.append(send(out_ref.at[slot], slot, side_send, side_recv, k + 1, side))
        pair_copies.append(send(out_ref.at[slot], slot, pair_send, pair_recv, k + 1, pair))
        side_copies[-1].start()
        pair_copies[-1].start()
    for k in range(outers):
        side_copies[k].wait_recv()
        slot = at((outer + outers - k) % outers, 1 - middle, inner)
        pair_copies.append(send(out_ref.at[slot], slot, pair_send, pair_recv, outers + k, pair))
        pair_copies[-1].start()
    for copy in pair_copies:
        copy.wait_recv()
    for copy in far_copies + side_copies + pair_copies:
        copy.wait_send()
    own.wait()


def spread(packed):
    devices = lax.axis_size("ctx")
    outers = devices // 4
    rows, columns = packed.shape
    gathered = pl.pallas_call(
        functools.partial(spread_kernel, devices),
        out_shape=jax.ShapeDtypeStruct((devices, rows, columns), packed.dtype),
        in_specs=[pl.BlockSpec(memory_space=pltpu.VMEM)],
        out_specs=pl.BlockSpec(memory_space=pltpu.VMEM),
        scratch_shapes=[
            pltpu.SemaphoreType.DMA((outers - 1,)),
            pltpu.SemaphoreType.DMA((outers - 1,)),
            pltpu.SemaphoreType.DMA((outers,)),
            pltpu.SemaphoreType.DMA((outers,)),
            pltpu.SemaphoreType.DMA((2 * outers,)),
            pltpu.SemaphoreType.DMA((2 * outers,)),
            pltpu.SemaphoreType.DMA,
        ],
        compiler_params=pltpu.CompilerParams(
            collective_id=0, has_side_effects=True, vmem_limit_bytes=24 * 1024 * 1024
        ),
        cost_estimate=pl.CostEstimate(flops=0, bytes_accessed=20 * packed.size * devices, transcendentals=0),
        name="spread",
    )(packed)
    return gathered.reshape(devices * rows, columns)


def hand_on(value, by):
    parts = lax.axis_size("groups")
    return lax.ppermute(value, "groups", [(i, (i + by) % parts) for i in range(parts)])


def local(query_states, key_states, value_rows, positions, out_weight):
    tokens, query_heads, head_size = query_states.shape
    kv_heads = key_states.shape[1]
    group = query_heads // kv_heads
    half = tokens // 2
    devices = lax.axis_size("ctx")
    blocks = 2 * devices
    parts = lax.axis_size("groups")
    me_part = lax.axis_index("groups")
    share = out_weight.shape[1] // parts
    weight_share = lax.dynamic_slice_in_dim(out_weight, me_part * share, share, 1)
    weight = lax.all_gather(weight_share, "ctx", axis=1, tiled=True)
    packed = jnp.concatenate(
        [key_states.reshape(tokens, kv_heads * head_size), value_rows.reshape(tokens, kv_heads * head_size)], axis=1
    )
    first = positions[0] // half
    firsts = lax.all_gather(first, "ctx")
    gathered = spread(packed)
    wanted = jnp.arange(blocks, dtype=jnp.int32)[:, None]
    stored = jnp.stack([firsts, blocks - 1 - firsts], axis=1).reshape(1, blocks)
    place = jnp.sum(jnp.where(stored == wanted, jnp.arange(blocks, dtype=jnp.int32)[None, :], 0), axis=1)
    place = place.astype(jnp.int32)
    own = jnp.stack([first, blocks - 1 - first]).astype(jnp.int32)
    query_parts = query_states.reshape(2, half, kv_heads, group, head_size).transpose(2, 0, 3, 1, 4)
    query_parts = query_parts.reshape(kv_heads, 2, group * half, head_size)
    pieces = min(2, kv_heads)
    span = kv_heads // pieces
    attended = [
        attend(query_parts[i * span : (i + 1) * span], gathered, place, own, i * span, kv_heads) for i in range(pieces)
    ]

    def project(rows):
        product = lax.dot_general(
            jnp.concatenate(rows, axis=0), weight, (((0,), (0,)), ((), ())), preferred_element_type=jnp.float32
        )
        return product.astype(jnp.bfloat16)

    guests = [[hand_on(piece, by) for piece in attended] for by in range(1, parts)]
    mine = project(attended)
    results = [mine] + [hand_on(project(rows), parts - 1 - i) for i, rows in enumerate(guests)]
    shares = jnp.stack([r.reshape(tokens, devices, share) for r in results])
    order = (jnp.arange(parts) - me_part) % parts
    if parts == 2:
        low = jnp.where(me_part == 0, shares[0], shares[1])
        high = jnp.where(me_part == 0, shares[1], shares[0])
        combined = jnp.stack([low, high], axis=2)
    else:
        combined = jnp.moveaxis(jnp.take(shares, order, axis=0), 0, 2)
    combined = combined.reshape(tokens, devices * parts * share)
    return lax.psum_scatter(combined, "tp", scatter_dimension=1, tiled=True)


def solution(mesh):
    in_specs = (
        P(("groups", "ctx"), "tp", None),
        P(("groups", "ctx"), "tp", None),
        P(("groups", "ctx"), "tp", None),
        P(("groups", "ctx")),
        P("tp", "ctx"),
    )
    out_specs = P(("groups", "ctx"), "tp")
    return jax.shard_map(local, mesh=mesh, in_specs=in_specs, out_specs=out_specs, check_vma=False)
```

time: 310 us -> 296 us (0.955); the launches traced: 305 us -> 296 us
  Pallas kernels: 0 us -> 188 us
  starting transfers between devices: 75.3 us -> 2.74 us
  matrix products: 77 us -> 16.8 us
  local copies, waits for them, and re-layouts: 53.5 us -> 15.3 us
  loops' own time: 19 us -> 0 us
  other arithmetic: 15.3 us -> 0.6 us
  blocking collectives: 0 us -> 13.1 us
  waiting for transfers between devices: 49.6 us -> 42.9 us
    pallas_call x0 -> x3, Pallas kernels: none -> 188 us  [the longest x1 120 us: spread(): pl.pallas_call(functools.partial(spread_kernel, devices), out_shape=jax.S...]
    ppermute x45 -> x3, starting transfers between devices: 75.3 us -> 2.7 us  [hand_on(): lax.ppermute(value, 'groups', [(i, (i + by) % parts) for i in range(parts)])]
    dot_general x63 -> x2, matrix products: 77 us -> 16.8 us  [project(): lax.dot_general(jnp.concatenate(rows, axis=0), weight, (((0,), (0,)), (()...]
    while x102 -> x0, local copies, waits for them, and re-layouts: 36.7 us -> none
    another operation x1 -> x0, loops' own time: 19 us -> none  [local(): lax.fori_loop(0, lax.axis_size('ctx') // 2 - 1, paired_turn, (own_block,...]
    reduce_sum x31 -> x1, other arithmetic: 13.9 us -> 0.11 us  [local(): jnp.sum(jnp.where(stored == wanted, jnp.arange(blocks, dtype=jnp.int32)[N...]
    unnamed x0 -> x1, blocking collectives: none -> 13.1 us
    slice x16 -> x2, local copies, waits for them, and re-layouts: 8.61 us -> 0.81 us  [the longest x1 0.57 us: local(): first = positions[0] // half]
  transfers between devices with their start and end apart: 46 -> 4, of which waited for: 19 -> 2; matrix products, arithmetic and copies ran while one was open for 37% -> 3% of each run, Pallas kernels for 0% -> 64%
where the time goes in v1:
time: 296 us
  Pallas kernels  188 us (64%)
  waiting for transfers between devices  42.9 us (14%)
  matrix products  16.8 us (6%)
  between operations  16.1 us (5%)
  local copies, waits for them, and re-layouts  15.3 us (5%)
  blocking collectives  13.1 us (4%)
    pallas_call x1, Pallas kernels, spread(): pl.pallas_call(functools.partial(spread_kernel, devices), out_shape=jax.S...  120 us
    pallas_call x2, Pallas kernels, attend(): pl.pallas_call(functools.partial(attend_kernel, half, group), out_shape=j...  68.1 us
    ppermute x3, waiting for transfers between devices, hand_on(): lax.ppermute(value, 'groups', [(i, (i + by) % parts) for i in range(parts)])  42.9 us
    dot_general x2, matrix products, project(): lax.dot_general(jnp.concatenate(rows, axis=0), weight, (((0,), (0,)), (()...  16.8 us
    unnamed x1, blocking collectives  13.1 us
  transfers between devices with their start and end apart: 4, of which 2 were waited for; matrix products, arithmetic and copies ran while one was open for 3% of the time, Pallas kernels for 64%

profile of v1, /device:TPU:24, one launch (start us, length us, event | category | flops | bytes accessed | tf_op | source)
XLA Modules:
  0.0 295.5 jit_solution(14725721775209364895)
XLA Ops:
  6.5 0.0 copy-start
  6.5 0.0 copy-start.6
  6.5 0.0 copy-start.5
  6.5 0.0 copy-start.3
  6.5 0.0 copy-start.2
  6.5 0.0 all-gather.2.cloned.1.call-start
  6.6 1.5 copy-done
  8.1 1.0 constant_dynamic-slice_fusion
  9.2 0.0 all-gather.2.cloned.1.call-update
  9.2 0.0 copy-done.5
  9.2 0.6 slice.15
  12.3 0.0 copy-done.6
  12.3 0.6 dynamic-slice
  12.9 0.7 dynamic-update-slice
  13.7 13.1 %all-reduce = s32[16]{0:T(128)S(1)} all-reduce(s32[16]{0:T(128)S(1)} %dynamic-update-slice), channel_id=1, replica_groups=mesh['groups'=2,'ctx'=16,'tp'=1] {'ctx'}, use_global_device_ids=true, to_apply=%add | all-reduce | flops 16 | bytes 128
  26.8 0.1 copy.12
  26.8 0.1 eq.20
  26.9 0.0 copy-done.3
  26.9 0.0 copy-done.2
  27.0 0.1 copy_bitcast_fusion.1
  27.0 0.1 pad_maximum_fusion.1.own_ref
  27.1 0.0 copy-start.1
  27.1 120.0 %spread.1 = bf16[16,256,1024]{2,1,0:T(8,128)(2,1)S(1)} custom-call(bf16[256,1024]{1,0:T(8,128)(2,1)S(1)} %pad_maximum_fusion.1.own_ref), custom_call_target="tpu_custom_call" | custom-call | bytes 83886080 | tf_op jit(solution)/shard_map/spread/pallas_call | solution.py:170
  147.1 0.0 copy-done.1
  147.1 0.8 copy.22
  147.9 0.1 pad_add_fusion.1.own_ref
  148.0 0.1 select_reduce_fusion.place_ref
  148.1 0.2 fusion.8
  148.4 33.5 %attend.2 = bf16[2048,256]{1,0:T(8,128)(2,1)S(1)} custom-call(s32[32]{0:T(128)S(1)} %select_reduce_fusion.place_ref, s32[2]{0:T(128)S(1)} %pad_add_fusion.1.own_ref, bf16[2,2,1024,128]{3,2,1,0:T(8,128)(2,1)S(1)} %bitcast.37, bf16[4096,1024]{1,0:T(8,128)(2,1)S(1)} %bitcast.32, bf16[4096,1024]{1,0:T(8,128)(2,1)S(1)} %bitcast.33), custom_call_target="tpu_custom_call" | custom-call | flops 4429185024 | bytes 8388608 | tf_op jit(solution)/shard_map/attend/pallas_call | solution.py:84
  181.9 1.5 collective-permute-start
  183.4 34.5 %attend.3 = bf16[2048,256]{1,0:T(8,128)(2,1)} custom-call(s32[32]{0:T(128)S(1)} %select_reduce_fusion.place_ref, s32[2]{0:T(128)S(1)} %pad_add_fusion.1.own_ref, bf16[2,2,1024,128]{3,2,1,0:T(8,128)(2,1)S(1)} %bitcast.36, bf16[4096,1024]{1,0:T(8,128)(2,1)S(1)} %bitcast.34, bf16[4096,1024]{1,0:T(8,128)(2,1)S(1)} %bitcast.35), custom_call_target="tpu_custom_call" | custom-call | flops 4429185024 | bytes 8388608 | tf_op jit(solution)/shard_map/attend/pallas_call | solution.py:84
  217.9 0.6 collective-permute-start.1
  218.5 0.0 collective-permute-done
  218.5 24.9 %collective-permute-done.1 = bf16[2048,256]{1,0:T(8,128)(2,1)} collective-permute-done((bf16[2048,256]{1,0:T(8,128)(2,1)}, bf16[2048,256]{1,0:T(8,128)(2,1)}, u32[]{:S(2)}, u32[]{:S(2)}) %collective-permute-start.1) | collective-permute-done | bytes 1048608 | tf_op jit(solution)/shard_map/ppermute | solution.py:195
  243.4 0.0 all-gather.2.cloned.1.call-done
  243.4 0.0 copy-start.4
  243.4 11.0 %convolution_convert_fusion = bf16[256,2048]{1,0:T(8,128)(2,1)S(1)} fusion(bf16[4096,2048]{1,0:T(8,128)(2,1)} %all-gather.2.cloned.1.call-done, bf16[2048,256]{1,0:T(8,128)(2,1)} %collective-permute-done.1, bf16[2048,256]{1,0:T(8,128)(2,1)} %collective-permute-done), kind=kOutput, calls=%fused_computation | convolution fusion | flops 4299685888 | bytes 19922944 | tf_op jit(solution)/shard_map/dot_general | solution.py:230
  254.5 0.6 collective-permute-start.2
  255.1 0.0 copy-done.4
  255.1 5.7 %convolution_convert_fusion.1 = bf16[256,2048]{1,0:T(8,128)(2,1)S(1)} fusion(bf16[4096,2048]{1,0:T(8,128)(2,1)S(1)} %copy-done.4, bf16[2048,256]{1,0:T(8,128)(2,1)} %attend.3, bf16[2048,256]{1,0:T(8,128)(2,1)S(1)} %attend.2), kind=kOutput, calls=%fused_computation.1 | convolution fusion | flops 4299685888 | bytes 19922944 | tf_op jit(solution)/shard_map/dot_general | solution.py:230
  260.8 18.0 %collective-permute-done.2 = bf16[256,2048]{1,0:T(8,128)(2,1)S(1)} collective-permute-done((bf16[256,2048]{1,0:T(8,128)(2,1)S(1)}, bf16[256,2048]{1,0:T(8,128)(2,1)S(1)}, u32[]{:S(2)}, u32[]{:S(2)}) %collective-permute-start.2) | collective-permute-done | bytes 1048608 | tf_op jit(solution)/shard_map/ppermute | solution.py:195
  278.8 0.1 select_bitcast_fusion.1
  279.0 0.2 copy.17
  279.2 0.2 copy.18
  279.4 0.2 pad_maximum_fusion
  279.6 4.6 %copy.14 = bf16[256,16,2,128]{3,2,1,0:T(2,128)(2,1)} copy(bf16[256,16,2,128]{3,1,0,2:T(8,128)(2,1)S(1)} %pad_maximum_fusion) | data formatting | bytes 4194304 | tf_op jit(solution)/shard_map/stack | solution.py:243
  284.2 4.5 %reshape.62 = bf16[256,4096]{1,0:T(8,128)(2,1)} reshape(bf16[256,16,2,128]{3,2,1,0:T(2,128)(2,1)} %copy.14) | data formatting | bytes 4194304 | tf_op jit(solution)/shard_map/reshape | solution.py:246
  (3 shorter events, 0.0 us)
Async XLA Ops:
  6.5 1.6 copy-start
  6.5 5.8 %copy-start.6 = (u32[32]{0:T(128)S(1)}, u32[32]{0:T(128)}, u32[]{:S(2)}) copy-start(u32[32]{0:T(128)} %constant.31) | copy-start | bytes 388
  6.5 2.7 copy-start.5
  6.5 20.4 %copy-start.3 = (bf16[256,4,128]{2,1,0:T(4,128)(2,1)S(1)}, bf16[256,4,128]{2,1,0:T(4,128)(2,1)}, u32[]{:S(2)}) copy-start(bf16[256,4,128]{2,1,0:T(4,128)(2,1)} %param.6) | copy-start | bytes 786436
  6.5 20.4 %copy-start.2 = (bf16[256,4,128]{2,1,0:T(4,128)(2,1)S(1)}, bf16[256,4,128]{2,1,0:T(4,128)(2,1)}, u32[]{:S(2)}) copy-start(bf16[256,4,128]{2,1,0:T(4,128)(2,1)} %param.7) | copy-start | bytes 786436
  6.5 236.9 %all-gather.2.cloned.1.call-start = ((), (), s32[]{:S(2)}) async-start(), calls=%async_computation | async-start | bytes 17825792 | tf_op jit(solution)/shard_map/all_gather | solution.py:209
  27.1 120.0 %copy-start.1 = (bf16[256,32,128]{2,1,0:T(8,128)(2,1)S(1)}, bf16[256,32,128]{2,1,0:T(8,128)(2,1)}, u32[]{:S(2)}) copy-start(bf16[256,32,128]{2,1,0:T(8,128)(2,1)} %param.5) | copy-start | bytes 6291460
  181.9 36.6 %collective-permute-start = (bf16[2048,256]{1,0:T(8,128)(2,1)S(1)}, bf16[2048,256]{1,0:T(8,128)(2,1)}, u32[]{:S(2)}, u32[]{:S(2)}) collective-permute-start(bf16[2048,256]{1,0:T(8,128)(2,1)S(1)} %attend.2), channel_id=1, source_target_pairs={{0,16},{16,0},{1,17},{17,1},{2,18},{18,2},{3,19},{19,3},{4,20},{20... | collective-permute-start | bytes 3145736 | tf_op jit(solution)/shard_map/ppermute | solution.py:195
  217.9 25.5 %collective-permute-start.1 = (bf16[2048,256]{1,0:T(8,128)(2,1)}, bf16[2048,256]{1,0:T(8,128)(2,1)}, u32[]{:S(2)}, u32[]{:S(2)}) collective-permute-start(bf16[2048,256]{1,0:T(8,128)(2,1)} %attend.3), channel_id=1, source_target_pairs={{0,16},{16,0},{1,17},{17,1},{2,18},{18,2},{3,19},{19,3},{4,20},{20... | collective-permute-start | bytes 3145736 | tf_op jit(solution)/shard_map/ppermute | solution.py:195
  243.4 11.7 %copy-start.4 = (bf16[4096,2048]{1,0:T(8,128)(2,1)S(1)}, bf16[4096,2048]{1,0:T(8,128)(2,1)}, u32[]{:S(2)}) copy-start(bf16[4096,2048]{1,0:T(8,128)(2,1)} %all-gather.2.cloned.1.call-done) | copy-start | bytes 50331652
  254.5 24.4 %collective-permute-start.2 = (bf16[256,2048]{1,0:T(8,128)(2,1)S(1)}, bf16[256,2048]{1,0:T(8,128)(2,1)S(1)}, u32[]{:S(2)}, u32[]{:S(2)}) collective-permute-start(bf16[256,2048]{1,0:T(8,128)(2,1)S(1)} %convolution_convert_fusion), channel_id=1, source_target_pairs={{0,16},{16,0},{1,17},{17,1},{2,18},{18,2},{3,19},{19,3},{4,20},{20... | collective-permute-start | bytes 3145736 | tf_op jit(solution)/shard_map/ppermute | solution.py:195
Sparse Core Ops, SparseCore 0:
  9.5 181.5 all-gather.1

commit v2 on v1

--- a/solution.py
+++ b/solution.py
@@ -10,7 +10,8 @@
 
 LOW_START = -1e30
 BLOCKS_PER_STEP = 4
-CHUNK = 256
+CHUNK = 1024
+TAIL = 16
 
 
 def attend_kernel(half, group, place_ref, own_ref, q_ref, k_ref, v_ref, out_ref, acc_ref, max_ref, sum_ref):
@@ -24,8 +25,8 @@
         keys, values = [], []
         for i in range(BLOCKS_PER_STEP):
             place = place_ref[number * BLOCKS_PER_STEP + i]
-            keys.append(k_ref[pl.ds(pl.multiple_of(place * half, half), half), :])
-            values.append(v_ref[pl.ds(pl.multiple_of(place * half, half), half), :])
+            keys.append(k_ref[pl.ds(pl.multiple_of(place, TAIL), half), :])
+            values.append(v_ref[pl.ds(pl.multiple_of(place, TAIL), half), :])
         key_part = jnp.concatenate(keys, axis=0)
         value_part = jnp.concatenate(values, axis=0)
         if masked:
@@ -74,11 +75,10 @@
             out_ref[pl.ds(g * head_size, head_size), pl.ds(which * half, half)] = attended.astype(jnp.bfloat16)
 
 
-def attend(query_parts, gathered, place, own, first_head, all_heads):
+def attend(query_parts, gathered, place, own, first_head, all_heads, half):
     kv_heads, _, rows, head_size = query_parts.shape
     keys_total = gathered.shape[0]
     blocks = place.shape[0]
-    half = keys_total // blocks
     group = rows // half
     flops = 4 * kv_heads * rows * head_size * half * (blocks + 1)
     return pl.pallas_call(
@@ -100,7 +100,7 @@
             ],
         ),
         compiler_params=pltpu.CompilerParams(
-            dimension_semantics=("arbitrary",), vmem_limit_bytes=40 * 1024 * 1024
+            dimension_semantics=("arbitrary",), vmem_limit_bytes=20 * 1024 * 1024
         ),
         cost_estimate=pl.CostEstimate(
             flops=flops, bytes_accessed=2 * gathered.size, transcendentals=flops // (4 * head_size)
@@ -187,12 +187,41 @@
         cost_estimate=pl.CostEstimate(flops=0, bytes_accessed=20 * packed.size * devices, transcendentals=0),
         name="spread",
     )(packed)
-    return gathered.reshape(devices * rows, columns)
+    return gathered
 
 
 def hand_on(value, by):
     parts = lax.axis_size("groups")
     return lax.ppermute(value, "groups", [(i, (i + by) % parts) for i in range(parts)])
+
+
+def weave_kernel(me_ref, *refs):
+    *shares, out_ref = refs
+    parts = len(shares)
+    share = shares[0].shape[1]
+    for p in range(parts):
+        by = lax.rem(p - me_ref[0] + parts, parts)
+        chosen = shares[0][...]
+        for k in range(1, parts):
+            chosen = jnp.where(by == k, shares[k][...], chosen)
+        out_ref[:, p * share : (p + 1) * share] = chosen
+
+
+def weave(results, me_part, devices):
+    parts = len(results)
+    tokens, columns = results[0].shape
+    share = columns // devices
+    return pl.pallas_call(
+        weave_kernel,
+        out_shape=jax.ShapeDtypeStruct((tokens, parts * columns), results[0].dtype),
+        grid_spec=pltpu.PrefetchScalarGridSpec(
+            num_scalar_prefetch=1,
+            grid=(devices,),
+            in_specs=[pl.BlockSpec((tokens, share), lambda i, *_: (0, i))] * parts,
+            out_specs=pl.BlockSpec((tokens, parts * share), lambda i, *_: (0, i)),
+        ),
+        name="weave",
+    )(me_part.astype(jnp.int32).reshape(1), *results)
 
 
 def local(query_states, key_states, value_rows, positions, out_weight):
@@ -206,16 +235,21 @@
     me_part = lax.axis_index("groups")
     share = out_weight.shape[1] // parts
     weight_share = lax.dynamic_slice_in_dim(out_weight, me_part * share, share, 1)
-    weight = lax.all_gather(weight_share, "ctx", axis=1, tiled=True)
     packed = jnp.concatenate(
         [key_states.reshape(tokens, kv_heads * head_size), value_rows.reshape(tokens, kv_heads * head_size)], axis=1
     )
     first = positions[0] // half
-    firsts = lax.all_gather(first, "ctx")
-    gathered = spread(packed)
+    tail = jnp.broadcast_to(first.astype(packed.dtype), (TAIL, packed.shape[1]))
+    gathered = spread(jnp.concatenate([packed, tail], axis=0))
+    firsts = gathered[:, tokens, 0].astype(jnp.int32)
+    firsts, weight_share = lax.optimization_barrier((firsts, weight_share))
+    weight = lax.all_gather(weight_share, "ctx", axis=1, tiled=True)
+    gathered = gathered.reshape(devices * (tokens + TAIL), packed.shape[1])
     wanted = jnp.arange(blocks, dtype=jnp.int32)[:, None]
     stored = jnp.stack([firsts, blocks - 1 - firsts], axis=1).reshape(1, blocks)
-    place = jnp.sum(jnp.where(stored == wanted, jnp.arange(blocks, dtype=jnp.int32)[None, :], 0), axis=1)
+    kept = jnp.arange(blocks, dtype=jnp.int32)[None, :]
+    starts = kept // 2 * (tokens + TAIL) + kept % 2 * half
+    place = jnp.sum(jnp.where(stored == wanted, starts, 0), axis=1)
     place = place.astype(jnp.int32)
     own = jnp.stack([first, blocks - 1 - first]).astype(jnp.int32)
     query_parts = query_states.reshape(2, half, kv_heads, group, head_size).transpose(2, 0, 3, 1, 4)
@@ -223,7 +257,7 @@
     pieces = min(2, kv_heads)
     span = kv_heads // pieces
     attended = [
-        attend(query_parts[i * span : (i + 1) * span], gathered, place, own, i * span, kv_heads) for i in range(pieces)
+        attend(query_parts[i * span : (i + 1) * span], gathered, place, own, i * span, kv_heads, half) for i in range(pieces)
     ]
 
     def project(rows):
@@ -235,15 +269,12 @@
     guests = [[hand_on(piece, by) for piece in attended] for by in range(1, parts)]
     mine = project(attended)
     results = [mine] + [hand_on(project(rows), parts - 1 - i) for i, rows in enumerate(guests)]
-    shares = jnp.stack([r.reshape(tokens, devices, share) for r in results])
-    order = (jnp.arange(parts) - me_part) % parts
-    if parts == 2:
-        low = jnp.where(me_part == 0, shares[0], shares[1])
-        high = jnp.where(me_part == 0, shares[1], shares[0])
-        combined = jnp.stack([low, high], axis=2)
+    if share % 128 == 0:
+        combined = weave(results, me_part, devices)
     else:
-        combined = jnp.moveaxis(jnp.take(shares, order, axis=0), 0, 2)
-    combined = combined.reshape(tokens, devices * parts * share)
+        shares = jnp.stack([r.reshape(tokens, devices, share) for r in results])
+        order = (jnp.arange(parts) - me_part) % parts
+        combined = jnp.moveaxis(jnp.take(shares, order, axis=0), 0, 2).reshape(tokens, devices * parts * share)
     return lax.psum_scatter(combined, "tp", scatter_dimension=1, tiled=True)
 
 

time: 296 us -> 280 us (0.946); the launches traced: 296 us -> 276 us
  Pallas kernels: 188 us -> 133 us
  waiting for transfers between devices: 42.9 us -> 91.7 us
  blocking collectives: 13.1 us -> 0 us
    all_gather x1, waiting for transfers between devices: 0.01 us -> 49.4 us  [local(): weight = lax.all_gather(weight_share, 'ctx', axis=1, tiled=True)]
    pallas_call x1, Pallas kernels: 120 us -> 78.2 us  [spread(): pl.pallas_call(functools.partial(spread_kernel, devices), out_shape=jax.S...]
    pallas_call x2, Pallas kernels: 68.1 us -> 45.3 us  [attend(): pl.pallas_call(functools.partial(attend_kernel, half, group), out_shape=j...]
    unnamed x1 -> x0, blocking collectives: 13.1 us -> none
    pallas_call x0 -> x1, Pallas kernels: none -> 9.41 us  [weave(): pl.pallas_call(weave_kernel, out_shape=jax.ShapeDtypeStruct((tokens, part...]
    unnamed x19 -> x14, local copies, waits for them, and re-layouts: 3.38 us -> 7.97 us
    another operation x1 -> x0, local copies, waits for them, and re-layouts: 4.57 us -> none  [local(): combined = jnp.stack([low, high], axis=2)]
    reshape x1 -> x0, local copies, waits for them, and re-layouts: 4.47 us -> none  [local(): combined = combined.reshape(tokens, devices * parts * share)]
  transfers between devices with their start and end apart: 4 -> 4, of which waited for: 2 -> 4; matrix products, arithmetic and copies ran while one was open for 3% -> 3% of each run, Pallas kernels for 64% -> 16%
where the time goes in v2:
time: 280 us; the launch traced here: 276 us
  Pallas kernels  133 us (48%)
  waiting for transfers between devices  91.7 us (33%)
  matrix products  16.5 us (6%)
  between operations  16.1 us (6%)
  local copies, waits for them, and re-layouts  14.3 us (5%)
  starting transfers between devices  3.71 us (1%)
    pallas_call x1, Pallas kernels, spread(): pl.pallas_call(functools.partial(spread_kernel, devices), out_shape=jax.S...  78.2 us
    all_gather x1, waiting for transfers between devices, local(): weight = lax.all_gather(weight_share, 'ctx', axis=1, tiled=True)  49.4 us
    pallas_call x2, Pallas kernels, attend(): pl.pallas_call(functools.partial(attend_kernel, half, group), out_shape=j...  45.3 us
    ppermute x3, waiting for transfers between devices, hand_on(): lax.ppermute(value, 'groups', [(i, (i + by) % parts) for i in range(parts)])  42.2 us
    dot_general x2, matrix products, project(): lax.dot_general(jnp.concatenate(rows, axis=0), weight, (((0,), (0,)), (()...  16.5 us
    pallas_call x1, Pallas kernels, weave(): pl.pallas_call(weave_kernel, out_shape=jax.ShapeDtypeStruct((tokens, part...  9.41 us
    unnamed x14, local copies, waits for them, and re-layouts  7.97 us
  transfers between devices with their start and end apart: 4, of which 4 were waited for; matrix products, arithmetic and copies ran while one was open for 3% of the time, Pallas kernels for 16%

profile of v2, /device:TPU:24, one launch (start us, length us, event | category | flops | bytes accessed | tf_op | source)
XLA Modules:
  0.0 275.8 jit_solution(12809565532757641102)
XLA Ops:
  6.5 0.0 copy-start
  6.5 0.0 all-gather.2.cloned.1.call-start
  6.5 1.3 slice.18
  10.5 1.1 copy_bitcast_fusion.1
  11.6 0.1 fusion.8.own_ref
  11.7 78.2 %spread.1 = bf16[16,272,1024]{2,1,0:T(8,128)(2,1)S(1)} custom-call(bf16[272,1024]{1,0:T(8,128)(2,1)S(1)} %fusion.8.own_ref), custom_call_target="tpu_custom_call" | custom-call | bytes 89128960 | tf_op jit(solution)/shard_map/spread/pallas_call | solution.py:170
  89.9 0.4 convert_reduce_fusion
  90.3 0.0 copy-start.1
  90.3 3.4 %copy-done.1 = bf16[16,272,1024]{2,1,0:T(8,128)(2,1)} copy-done((bf16[16,272,1024]{2,1,0:T(8,128)(2,1)}, bf16[16,272,1024]{2,1,0:T(8,128)(2,1)S(1)}, u32[]{:S(2)}) %copy-start.1) | copy-done | bytes 8912920
  93.7 0.0 copy-done
  93.7 1.0 constant_dynamic-slice_fusion
  94.8 0.0 all-gather.2.cloned.1.call-update
  94.8 0.1 copy.10
  94.9 0.1 eq.17
  95.0 2.4 copy.17
  97.4 0.1 pad_add_fusion.1.own_ref
  97.5 0.1 select_reduce_fusion.place_ref
  97.6 0.2 fusion.14
  97.9 0.0 copy-start.2
  97.9 3.5 %copy-done.2 = bf16[16,272,1024]{2,1,0:T(8,128)(2,1)S(1)} copy-done((bf16[16,272,1024]{2,1,0:T(8,128)(2,1)S(1)}, bf16[16,272,1024]{2,1,0:T(8,128)(2,1)}, u32[]{:S(2)}) %copy-start.2) | copy-done | bytes 8912920
  101.4 22.5 %attend.2 = bf16[2048,256]{1,0:T(8,128)(2,1)S(1)} custom-call(s32[32]{0:T(128)S(1)} %select_reduce_fusion.place_ref, s32[2]{0:T(128)S(1)} %pad_add_fusion.1.own_ref, bf16[2,2,1024,128]{3,2,1,0:T(8,128)(2,1)S(1)} %bitcast.27, bf16[4352,1024]{1,0:T(8,128)(2,1)S(1)} %bitcast.22, bf16[4352,1024]{1,0:T(8,128)(2,1)S(1)} %bitcast.23), custom_call_target="tpu_custom_call" | custom-call | flops 4429185024 | bytes 8912896 | tf_op jit(solution)/shard_map/attend/pallas_call | solution.py:84
  123.9 1.6 collective-permute-start
  125.5 22.7 %attend.3 = bf16[2048,256]{1,0:T(8,128)(2,1)S(1)} custom-call(s32[32]{0:T(128)S(1)} %select_reduce_fusion.place_ref, s32[2]{0:T(128)S(1)} %pad_add_fusion.1.own_ref, bf16[2,2,1024,128]{3,2,1,0:T(8,128)(2,1)S(1)} %bitcast.26, bf16[4352,1024]{1,0:T(8,128)(2,1)S(1)} %bitcast.24, bf16[4352,1024]{1,0:T(8,128)(2,1)S(1)} %bitcast.25), custom_call_target="tpu_custom_call" | custom-call | flops 4429185024 | bytes 8912896 | tf_op jit(solution)/shard_map/attend/pallas_call | solution.py:84
  148.2 0.0 copy-start.3
  148.2 0.6 collective-permute-start.1
  148.8 0.6 collective-permute-done
  149.5 0.0 copy-done.3
  149.5 0.0 copy-start.6
  149.5 1.0 copy-done.6
  150.4 23.1 %collective-permute-done.1 = bf16[2048,256]{1,0:T(8,128)(2,1)} collective-permute-done((bf16[2048,256]{1,0:T(8,128)(2,1)S(1)}, bf16[2048,256]{1,0:T(8,128)(2,1)}, u32[]{:S(2)}, u32[]{:S(2)}) %collective-permute-start.1) | collective-permute-done | bytes 1048608 | tf_op jit(solution)/shard_map/ppermute | solution.py:195
  173.6 49.4 %all-gather.2.cloned.1.call-done = bf16[4096,2048]{1,0:T(8,128)(2,1)} async-done(((bf16[4096,128]{1,0:T(8,128)(2,1)}), bf16[4096,2048]{1,0:T(8,128)(2,1)}) %all-gather.2.cloned.1.call-update) | async-done | bytes 16777232 | tf_op jit(solution)/shard_map/all_gather | solution.py:246
  223.0 0.0 copy-start.4
  223.0 0.0 copy-start.5
  223.0 11.0 %convolution_convert_fusion = bf16[256,2048]{1,0:T(8,128)(2,1)S(1)} fusion(bf16[4096,2048]{1,0:T(8,128)(2,1)} %all-gather.2.cloned.1.call-done, bf16[2048,256]{1,0:T(8,128)(2,1)} %collective-permute-done.1, bf16[2048,256]{1,0:T(8,128)(2,1)} %copy-done.6), kind=kOutput, calls=%fused_computation | convolution fusion | flops 4299685888 | bytes 19922944 | tf_op jit(solution)/shard_map/dot_general | solution.py:264
  234.1 1.5 collective-permute-start.2
  235.6 0.0 copy-done.4
  235.6 0.0 copy-done.5
  235.6 5.5 %convolution_convert_fusion.1.refs_0_ = bf16[256,2048]{1,0:T(8,128)(2,1)} fusion(bf16[4096,2048]{1,0:T(8,128)(2,1)S(1)} %copy-done.5, bf16[2048,256]{1,0:T(8,128)(2,1)S(1)} %copy-done.4, bf16[2048,256]{1,0:T(8,128)(2,1)S(1)} %attend.2), kind=kOutput, calls=%fused_computation.1 | convolution fusion | flops 4299685888 | bytes 19922944 | tf_op jit(solution)/shard_map/dot_general | solution.py:264
  241.1 18.5 %collective-permute-done.2.refs_1_ = bf16[256,2048]{1,0:T(8,128)(2,1)} collective-permute-done((bf16[256,2048]{1,0:T(8,128)(2,1)S(1)}, bf16[256,2048]{1,0:T(8,128)(2,1)}, u32[]{:S(2)}, u32[]{:S(2)}) %collective-permute-start.2) | collective-permute-done | bytes 1048608 | tf_op jit(solution)/shard_map/ppermute | solution.py:195
  259.5 9.4 %weave.1 = bf16[256,4096]{1,0:T(8,128)(2,1)} custom-call(s32[1]{0:T(128)} %bitcast.me_ref, bf16[256,2048]{1,0:T(8,128)(2,1)} %convolution_convert_fusion.1.refs_0_, bf16[256,2048]{1,0:T(8,128)(2,1)} %collective-permute-done.2.refs_1_), custom_call_target="tpu_custom_call" | custom-call | tf_op jit(solution)/shard_map/weave/pallas_call | solution.py:214
  (3 shorter events, 0.0 us)
Async XLA Ops:
  6.5 87.2 %copy-start = (bf16[4096,256]{1,0:T(8,128)(2,1)S(1)}, bf16[4096,256]{1,0:T(8,128)(2,1)}, u32[]{:S(2)}) copy-start(bf16[4096,256]{1,0:T(8,128)(2,1)} %param.9) | copy-start | bytes 6291460
  6.5 216.5 %all-gather.2.cloned.1.call-start = ((), (), s32[]{:S(2)}) async-start(), calls=%async_computation | async-start | bytes 17825792 | tf_op jit(solution)/shard_map/all_gather | solution.py:246
  90.3 3.5 %copy-start.1 = (bf16[16,272,1024]{2,1,0:T(8,128)(2,1)}, bf16[16,272,1024]{2,1,0:T(8,128)(2,1)S(1)}, u32[]{:S(2)}) copy-start(bf16[16,272,1024]{2,1,0:T(8,128)(2,1)S(1)} %spread.1) | copy-start | bytes 26738692
  97.9 3.5 %copy-start.2 = (bf16[16,272,1024]{2,1,0:T(8,128)(2,1)S(1)}, bf16[16,272,1024]{2,1,0:T(8,128)(2,1)}, u32[]{:S(2)}) copy-start(bf16[16,272,1024]{2,1,0:T(8,128)(2,1)} %copy-done.1) | copy-start | bytes 26738692
  123.9 25.5 %collective-permute-start = (bf16[2048,256]{1,0:T(8,128)(2,1)S(1)}, bf16[2048,256]{1,0:T(8,128)(2,1)S(1)}, u32[]{:S(2)}, u32[]{:S(2)}) collective-permute-start(bf16[2048,256]{1,0:T(8,128)(2,1)S(1)} %attend.2), channel_id=1, source_target_pairs={{0,16},{16,0},{1,17},{17,1},{2,18},{18,2},{3,19},{19,3},{4,20},{20... | collective-permute-start | bytes 3145736 | tf_op jit(solution)/shard_map/ppermute | solution.py:195
  148.2 1.2 copy-start.3
  148.2 25.4 %collective-permute-start.1 = (bf16[2048,256]{1,0:T(8,128)(2,1)S(1)}, bf16[2048,256]{1,0:T(8,128)(2,1)}, u32[]{:S(2)}, u32[]{:S(2)}) collective-permute-start(bf16[2048,256]{1,0:T(8,128)(2,1)S(1)} %attend.3), channel_id=1, source_target_pairs={{0,16},{16,0},{1,17},{17,1},{2,18},{18,2},{3,19},{19,3},{4,20},{20... | collective-permute-start | bytes 3145736 | tf_op jit(solution)/shard_map/ppermute | solution.py:195
  149.5 1.0 copy-start.6
  223.0 12.6 %copy-start.4 = (bf16[2048,256]{1,0:T(8,128)(2,1)S(1)}, bf16[2048,256]{1,0:T(8,128)(2,1)}, u32[]{:S(2)}) copy-start(bf16[2048,256]{1,0:T(8,128)(2,1)} %copy-done.3) | copy-start | bytes 3145732
  223.0 12.6 %copy-start.5 = (bf16[4096,2048]{1,0:T(8,128)(2,1)S(1)}, bf16[4096,2048]{1,0:T(8,128)(2,1)}, u32[]{:S(2)}) copy-start(bf16[4096,2048]{1,0:T(8,128)(2,1)} %all-gather.2.cloned.1.call-done) | copy-start | bytes 50331652
  234.1 25.5 %collective-permute-start.2 = (bf16[256,2048]{1,0:T(8,128)(2,1)S(1)}, bf16[256,2048]{1,0:T(8,128)(2,1)}, u32[]{:S(2)}, u32[]{:S(2)}) collective-permute-start(bf16[256,2048]{1,0:T(8,128)(2,1)S(1)} %convolution_convert_fusion), channel_id=1, source_target_pairs={{0,16},{16,0},{1,17},{17,1},{2,18},{18,2},{3,19},{19,3},{4,20},{20... | collective-permute-start | bytes 3145736 | tf_op jit(solution)/shard_map/ppermute | solution.py:195
Sparse Core Ops, SparseCore 0:
  94.9 128.0 all-gather.1

commit v3 on v2

--- a/solution.py
+++ b/solution.py
@@ -195,16 +195,16 @@
     return lax.ppermute(value, "groups", [(i, (i + by) % parts) for i in range(parts)])
 
 
-def weave_kernel(me_ref, *refs):
+def weave_kernel(share, me_ref, *refs):
     *shares, out_ref = refs
     parts = len(shares)
-    share = shares[0].shape[1]
     for p in range(parts):
         by = lax.rem(p - me_ref[0] + parts, parts)
         chosen = shares[0][...]
         for k in range(1, parts):
             chosen = jnp.where(by == k, shares[k][...], chosen)
-        out_ref[:, p * share : (p + 1) * share] = chosen
+        for i in range(chosen.shape[1] // share):
+            out_ref[:, (i * parts + p) * share : (i * parts + p + 1) * share] = chosen[:, i * share : (i + 1) * share]
 
 
 def weave(results, me_part, devices):
@@ -212,13 +212,13 @@
     tokens, columns = results[0].shape
     share = columns // devices
     return pl.pallas_call(
-        weave_kernel,
+        functools.partial(weave_kernel, share),
         out_shape=jax.ShapeDtypeStruct((tokens, parts * columns), results[0].dtype),
         grid_spec=pltpu.PrefetchScalarGridSpec(
             num_scalar_prefetch=1,
-            grid=(devices,),
-            in_specs=[pl.BlockSpec((tokens, share), lambda i, *_: (0, i))] * parts,
-            out_specs=pl.BlockSpec((tokens, parts * share), lambda i, *_: (0, i)),
+            grid=(devices // 4,),
+            in_specs=[pl.BlockSpec((tokens, 4 * share), lambda i, *_: (0, i))] * parts,
+            out_specs=pl.BlockSpec((tokens, 4 * parts * share), lambda i, *_: (0, i)),
         ),
         name="weave",
     )(me_part.astype(jnp.int32).reshape(1), *results)
@@ -235,6 +235,7 @@
     me_part = lax.axis_index("groups")
     share = out_weight.shape[1] // parts
     weight_share = lax.dynamic_slice_in_dim(out_weight, me_part * share, share, 1)
+    weight = lax.all_gather(weight_share, "ctx", axis=1, tiled=True)
     packed = jnp.concatenate(
         [key_states.reshape(tokens, kv_heads * head_size), value_rows.reshape(tokens, kv_heads * head_size)], axis=1
     )
@@ -242,8 +243,6 @@
     tail = jnp.broadcast_to(first.astype(packed.dtype), (TAIL, packed.shape[1]))
     gathered = spread(jnp.concatenate([packed, tail], axis=0))
     firsts = gathered[:, tokens, 0].astype(jnp.int32)
-    firsts, weight_share = lax.optimization_barrier((firsts, weight_share))
-    weight = lax.all_gather(weight_share, "ctx", axis=1, tiled=True)
     gathered = gathered.reshape(devices * (tokens + TAIL), packed.shape[1])
     wanted = jnp.arange(blocks, dtype=jnp.int32)[:, None]
     stored = jnp.stack([firsts, blocks - 1 - firsts], axis=1).reshape(1, blocks)

time: 280 us -> 271 us (0.968); the launches traced: 276 us -> 271 us
  waiting for transfers between devices: 91.7 us -> 42.2 us
  Pallas kernels: 133 us -> 179 us
    pallas_call x1, Pallas kernels: 78.2 us -> 130 us  [spread(): pl.pallas_call(functools.partial(spread_kernel, devices), out_shape=jax.S...]
    all_gather x1, waiting for transfers between devices: 49.4 us -> 0.01 us  [local(): weight = lax.all_gather(weight_share, 'ctx', axis=1, tiled=True)]
    pallas_call x1, Pallas kernels: 9.41 us -> 3.89 us  [weave(): pl.pallas_call(functools.partial(weave_kernel, share), out_shape=jax.Shap...]
    unnamed x14 -> x20, local copies, waits for them, and re-layouts: 7.97 us -> 9.5 us
  transfers between devices with their start and end apart: 4 -> 4, of which waited for: 4 -> 3; matrix products, arithmetic and copies ran while one was open for 3% -> 4% of each run, Pallas kernels for 16% -> 65%
where the time goes in v3:
time: 271 us
  Pallas kernels  179 us (66%)
  waiting for transfers between devices  42.2 us (16%)
  matrix products  16.5 us (6%)
  between operations  16.1 us (6%)
  local copies, waits for them, and re-layouts  14 us (5%)
  starting transfers between devices  2.71 us (1%)
    pallas_call x1, Pallas kernels, spread(): pl.pallas_call(functools.partial(spread_kernel, devices), out_shape=jax.S...  130 us
    pallas_call x2, Pallas kernels, attend(): pl.pallas_call(functools.partial(attend_kernel, half, group), out_shape=j...  45.3 us
    ppermute x3, waiting for transfers between devices, hand_on(): lax.ppermute(value, 'groups', [(i, (i + by) % parts) for i in range(parts)])  42.2 us
    dot_general x2, matrix products, project(): lax.dot_general(jnp.concatenate(rows, axis=0), weight, (((0,), (0,)), (()...  16.5 us
    unnamed x20, local copies, waits for them, and re-layouts  9.5 us
  transfers between devices with their start and end apart: 4, of which 3 were waited for; matrix products, arithmetic and copies ran while one was open for 4% of the time, Pallas kernels for 65%

profile of v3, /device:TPU:24, one launch (start us, length us, event | category | flops | bytes accessed | tf_op | source)
XLA Modules:
  0.0 270.9 jit_solution(68544719613618603)
XLA Ops:
  6.5 0.0 copy-start
  6.5 0.0 copy-start.9
  6.5 0.0 copy-start.6
  6.5 0.0 copy-start.5
  6.5 0.0 all-gather.2.cloned.1.call-start
  6.6 1.5 copy-done
  8.1 1.0 constant_dynamic-slice_fusion
  9.2 0.0 all-gather.2.cloned.1.call-update
  9.2 0.0 copy-done.9
  9.2 0.6 slice.18
  12.3 0.0 copy-done.6
  12.3 0.0 copy-done.5
  12.3 0.1 copy_bitcast_fusion.1
  12.4 0.1 fusion.8.own_ref
  12.5 129.6 %spread.1 = bf16[16,272,1024]{2,1,0:T(8,128)(2,1)S(1)} custom-call(bf16[272,1024]{1,0:T(8,128)(2,1)S(1)} %fusion.8.own_ref), custom_call_target="tpu_custom_call" | custom-call | bytes 89128960 | tf_op jit(solution)/shard_map/spread/pallas_call | solution.py:170
  142.0 0.4 convert_reduce_fusion
  142.4 0.0 copy-start.1
  142.4 3.4 %copy-done.1 = bf16[16,272,1024]{2,1,0:T(8,128)(2,1)} copy-done((bf16[16,272,1024]{2,1,0:T(8,128)(2,1)}, bf16[16,272,1024]{2,1,0:T(8,128)(2,1)S(1)}, u32[]{:S(2)}) %copy-start.1) | copy-done | bytes 8912920
  145.9 0.1 copy.10
  146.0 0.1 eq.17
  146.1 2.4 copy.17
  148.5 0.1 pad_add_fusion.1.own_ref
  148.6 0.1 select_reduce_fusion.place_ref
  148.7 0.2 fusion.14
  148.9 0.0 copy-start.2
  148.9 3.5 %copy-done.2 = bf16[16,272,1024]{2,1,0:T(8,128)(2,1)S(1)} copy-done((bf16[16,272,1024]{2,1,0:T(8,128)(2,1)S(1)}, bf16[16,272,1024]{2,1,0:T(8,128)(2,1)}, u32[]{:S(2)}) %copy-start.2) | copy-done | bytes 8912920
  152.5 22.5 %attend.2 = bf16[2048,256]{1,0:T(8,128)(2,1)S(1)} custom-call(s32[32]{0:T(128)S(1)} %select_reduce_fusion.place_ref, s32[2]{0:T(128)S(1)} %pad_add_fusion.1.own_ref, bf16[2,2,1024,128]{3,2,1,0:T(8,128)(2,1)S(1)} %bitcast.26, bf16[4352,1024]{1,0:T(8,128)(2,1)S(1)} %bitcast.21, bf16[4352,1024]{1,0:T(8,128)(2,1)S(1)} %bitcast.22), custom_call_target="tpu_custom_call" | custom-call | flops 4429185024 | bytes 8912896 | tf_op jit(solution)/shard_map/attend/pallas_call | solution.py:84
  175.0 1.6 collective-permute-start
  176.6 22.7 %attend.3 = bf16[2048,256]{1,0:T(8,128)(2,1)S(1)} custom-call(s32[32]{0:T(128)S(1)} %select_reduce_fusion.place_ref, s32[2]{0:T(128)S(1)} %pad_add_fusion.1.own_ref, bf16[2,2,1024,128]{3,2,1,0:T(8,128)(2,1)S(1)} %bitcast.25, bf16[4352,1024]{1,0:T(8,128)(2,1)S(1)} %bitcast.23, bf16[4352,1024]{1,0:T(8,128)(2,1)S(1)} %bitcast.24), custom_call_target="tpu_custom_call" | custom-call | flops 4429185024 | bytes 8912896 | tf_op jit(solution)/shard_map/attend/pallas_call | solution.py:84
  199.3 0.0 copy-start.3
  199.3 0.5 collective-permute-start.1
  199.9 0.6 collective-permute-done
  200.5 0.0 copy-done.3
  200.5 0.0 copy-start.8
  200.5 1.0 copy-done.8
  201.5 23.2 %collective-permute-done.1 = bf16[2048,256]{1,0:T(8,128)(2,1)} collective-permute-done((bf16[2048,256]{1,0:T(8,128)(2,1)S(1)}, bf16[2048,256]{1,0:T(8,128)(2,1)}, u32[]{:S(2)}, u32[]{:S(2)}) %collective-permute-start.1) | collective-permute-done | bytes 1048608 | tf_op jit(solution)/shard_map/ppermute | solution.py:195
  224.7 0.0 all-gather.2.cloned.1.call-done
  224.7 0.0 copy-start.4
  224.7 0.0 copy-start.7
  224.7 11.0 %convolution_convert_fusion = bf16[256,2048]{1,0:T(8,128)(2,1)S(1)} fusion(bf16[4096,2048]{1,0:T(8,128)(2,1)} %all-gather.2.cloned.1.call-done, bf16[2048,256]{1,0:T(8,128)(2,1)} %collective-permute-done.1, bf16[2048,256]{1,0:T(8,128)(2,1)} %copy-done.8), kind=kOutput, calls=%fused_computation | convolution fusion | flops 4299685888 | bytes 19922944 | tf_op jit(solution)/shard_map/dot_general | solution.py:263
  235.7 0.6 collective-permute-start.2
  236.3 0.0 copy-done.4
  236.3 0.0 copy-done.7
  236.3 5.5 %convolution_convert_fusion.1.refs_0_ = bf16[256,2048]{1,0:T(8,128)(2,1)} fusion(bf16[4096,2048]{1,0:T(8,128)(2,1)S(1)} %copy-done.7, bf16[2048,256]{1,0:T(8,128)(2,1)S(1)} %copy-done.4, bf16[2048,256]{1,0:T(8,128)(2,1)S(1)} %attend.2), kind=kOutput, calls=%fused_computation.1 | convolution fusion | flops 4299685888 | bytes 19922944 | tf_op jit(solution)/shard_map/dot_general | solution.py:263
  241.8 18.4 %collective-permute-done.2.refs_1_ = bf16[256,2048]{1,0:T(8,128)(2,1)} collective-permute-done((bf16[256,2048]{1,0:T(8,128)(2,1)S(1)}, bf16[256,2048]{1,0:T(8,128)(2,1)}, u32[]{:S(2)}, u32[]{:S(2)}) %collective-permute-start.2) | collective-permute-done | bytes 1048608 | tf_op jit(solution)/shard_map/ppermute | solution.py:195
  260.2 3.9 %weave.1 = bf16[256,4096]{1,0:T(8,128)(2,1)} custom-call(s32[1]{0:T(128)} %bitcast.me_ref, bf16[256,2048]{1,0:T(8,128)(2,1)} %convolution_convert_fusion.1.refs_0_, bf16[256,2048]{1,0:T(8,128)(2,1)} %collective-permute-done.2.refs_1_), custom_call_target="tpu_custom_call" | custom-call | tf_op jit(solution)/shard_map/weave/pallas_call | solution.py:214
  (3 shorter events, 0.0 us)
Async XLA Ops:
  6.5 1.6 copy-start
  6.5 2.7 copy-start.9
  6.5 5.8 %copy-start.6 = (bf16[256,4,128]{2,1,0:T(4,128)(2,1)S(1)}, bf16[256,4,128]{2,1,0:T(4,128)(2,1)}, u32[]{:S(2)}) copy-start(bf16[256,4,128]{2,1,0:T(4,128)(2,1)} %param.6) | copy-start | bytes 786436
  6.5 5.8 %copy-start.5 = (bf16[256,4,128]{2,1,0:T(4,128)(2,1)S(1)}, bf16[256,4,128]{2,1,0:T(4,128)(2,1)}, u32[]{:S(2)}) copy-start(bf16[256,4,128]{2,1,0:T(4,128)(2,1)} %param.7) | copy-start | bytes 786436
  6.5 218.1 %all-gather.2.cloned.1.call-start = ((), (), s32[]{:S(2)}) async-start(), calls=%async_computation | async-start | bytes 17825792 | tf_op jit(solution)/shard_map/all_gather | solution.py:238
  142.4 3.4 %copy-start.1 = (bf16[16,272,1024]{2,1,0:T(8,128)(2,1)}, bf16[16,272,1024]{2,1,0:T(8,128)(2,1)S(1)}, u32[]{:S(2)}) copy-start(bf16[16,272,1024]{2,1,0:T(8,128)(2,1)S(1)} %spread.1) | copy-start | bytes 26738692
  148.9 3.5 %copy-start.2 = (bf16[16,272,1024]{2,1,0:T(8,128)(2,1)S(1)}, bf16[16,272,1024]{2,1,0:T(8,128)(2,1)}, u32[]{:S(2)}) copy-start(bf16[16,272,1024]{2,1,0:T(8,128)(2,1)} %copy-done.1) | copy-start | bytes 26738692
  175.0 25.5 %collective-permute-start = (bf16[2048,256]{1,0:T(8,128)(2,1)S(1)}, bf16[2048,256]{1,0:T(8,128)(2,1)S(1)}, u32[]{:S(2)}, u32[]{:S(2)}) collective-permute-start(bf16[2048,256]{1,0:T(8,128)(2,1)S(1)} %attend.2), channel_id=1, source_target_pairs={{0,16},{16,0},{1,17},{17,1},{2,18},{18,2},{3,19},{19,3},{4,20},{20... | collective-permute-start | bytes 3145736 | tf_op jit(solution)/shard_map/ppermute | solution.py:195
  199.3 1.2 copy-start.3
  199.3 25.3 %collective-permute-start.1 = (bf16[2048,256]{1,0:T(8,128)(2,1)S(1)}, bf16[2048,256]{1,0:T(8,128)(2,1)}, u32[]{:S(2)}, u32[]{:S(2)}) collective-permute-start(bf16[2048,256]{1,0:T(8,128)(2,1)S(1)} %attend.3), channel_id=1, source_target_pairs={{0,16},{16,0},{1,17},{17,1},{2,18},{18,2},{3,19},{19,3},{4,20},{20... | collective-permute-start | bytes 3145736 | tf_op jit(solution)/shard_map/ppermute | solution.py:195
  200.5 1.0 copy-start.8
  224.7 11.6 %copy-start.4 = (bf16[2048,256]{1,0:T(8,128)(2,1)S(1)}, bf16[2048,256]{1,0:T(8,128)(2,1)}, u32[]{:S(2)}) copy-start(bf16[2048,256]{1,0:T(8,128)(2,1)} %copy-done.3) | copy-start | bytes 3145732
  224.7 11.6 %copy-start.7 = (bf16[4096,2048]{1,0:T(8,128)(2,1)S(1)}, bf16[4096,2048]{1,0:T(8,128)(2,1)}, u32[]{:S(2)}) copy-start(bf16[4096,2048]{1,0:T(8,128)(2,1)} %all-gather.2.cloned.1.call-done) | copy-start | bytes 50331652
  235.7 24.5 %collective-permute-start.2 = (bf16[256,2048]{1,0:T(8,128)(2,1)S(1)}, bf16[256,2048]{1,0:T(8,128)(2,1)}, u32[]{:S(2)}, u32[]{:S(2)}) collective-permute-start(bf16[256,2048]{1,0:T(8,128)(2,1)S(1)} %convolution_convert_fusion), channel_id=1, source_target_pairs={{0,16},{16,0},{1,17},{17,1},{2,18},{18,2},{3,19},{19,3},{4,20},{20... | collective-permute-start | bytes 3145736 | tf_op jit(solution)/shard_map/ppermute | solution.py:195
Sparse Core Ops, SparseCore 0:
  9.5 180.1 all-gather.1
